TPU v7x, 512 devices: a 4x2x32 block of a 4x8x32 slice. The times are simulated.
512 devices in a mesh: groups: 2 (over y), expert: 32 (over z), tensor: 8 (over x, core).
Axes of the slice: x: 4, y: 2, z: 32, core: 2. Of those that a mesh axis runs over, the one named last changes fastest.
The devices are a block of a 4x8x32 slice.
Arguments:
- tokens: bfloat16 [8192, 7168], P(('groups', 'expert'), 'tensor'), parts along dimension 0, may hold values from -6 to 6
- choices: int32 [8192, 4], P(('groups', 'expert')), parts along dimension 0, may hold values from 0 to 15, all different within a row; in each aligned block of 128 rows (0 to 127, 128 to 255, ...) at most 48 rows name the same one
- affinity: float32 [8192, 4], P(('groups', 'expert')), parts along dimension 0, may hold values from -6 to 6
- expert_gate: bfloat16 [7168, 16384], P('tensor', 'expert'), may hold values from -0.0625 to 0.0625
- expert_up: bfloat16 [7168, 16384], P('tensor', 'expert'), may hold values from -0.0625 to 0.0625
- expert_down: bfloat16 [16384, 7168], P('expert', 'tensor'), may hold values from -0.1875 to 0.1875
- shared_in: bfloat16 [2, 1024, 7168], P(None, 'expert', 'tensor'), may hold values from -0.0625 to 0.0625
- shared_down: bfloat16 [1024, 7168], P('expert', 'tensor'), may hold values from -0.1875 to 0.1875
Outputs:
- mixed: bfloat16 [8192, 7168], P(('groups', 'expert'), 'tensor'), parts along dimension 0
There are 2 independent parts, one for each index of `groups`. A program takes and returns all parts, laid end to end along the dimension named above; an argument that names none is the same for every part. Nothing has to cross between parts.
Inputs may be any that keep to these rules, and one draw needn't show every extreme that they name: `choices`: within the rows of one index of expert (128 tokens) every expert is named at most 48 times, a bound that some block reaches; a token names 4 different experts.
All inputs are finite; a program needn't handle non-finite values.
Results may differ from a plain program's by a relative error of at most 0.02.
Values may be sent and summed in bfloat16 or wider, within the bound.
No kernel may reach another device: no remote copies, remote signals or barrier semaphores. Data moves between devices by JAX's collectives and lax.ppermute only.
A program may use at most 64 MiB of HBM per device.

v0:
```python
import jax
import jax.numpy as jnp
from jax import lax
from jax.sharding import PartitionSpec as P


FFE = 1024
CAP = 48
CORES = 2
BF = jnp.bfloat16
F32 = jnp.float32


def dot(spec, a, b):
    return jnp.einsum(spec, a, b, preferred_element_type=F32)


def route(info, columns, top):
    tok = info.shape[2]
    own = (lax.axis_index("expert") * columns // FFE).astype(F32)
    hit = info[:, :top, :] == own
    named = jnp.any(hit, axis=1)
    weight = jnp.sum(jnp.where(hit, info[:, top:, :], 0.0), axis=1)
    order = jnp.arange(tok)
    before = (order[:, None] < order[None, :]).astype(BF)
    position = dot("ns,st->nt", named.astype(BF), before).astype(jnp.int32)
    return jnp.where(named, position, -1), weight


def local(tokens, choices, affinity, expert_gate, expert_up, expert_down, shared_in, shared_down):
    tok, width = tokens.shape
    columns = expert_gate.shape[1]
    units = shared_in.shape[1]
    top = choices.shape[1]
    blocks = lax.axis_size("expert")
    parts = lax.axis_size("tensor")
    pieces = FFE // columns
    near = blocks // pieces
    chips = parts // CORES
    half = CAP // CORES
    core = lax.axis_index("tensor") % CORES
    rings = [[r + pieces * k for k in range(near)] for r in range(pieces)]
    crosses = [[c + CORES * k for k in range(chips)] for c in range(CORES)]
    partner = [(t, t - t % CORES + (t + 1) % CORES) for t in range(parts)]

    def with_mates(array):
        moved = [
            lax.ppermute(
                array, "expert", [(z, z - z % pieces + (z + shift) % pieces) for z in range(blocks)]
            )
            for shift in range(1, pieces)
        ]
        return [array] + moved

    everyone = lax.all_gather(tokens, "expert", axis=0, tiled=True, axis_index_groups=rings)
    gates = with_mates(expert_gate)
    ups = with_mates(expert_up)
    small = with_mates(jnp.concatenate([shared_in.reshape(2 * units, width), shared_down], axis=0))
    sigmoids = jax.nn.sigmoid(affinity)
    mix = 2.5 * sigmoids / jnp.sum(sigmoids, axis=1, keepdims=True)
    info = jnp.concatenate([choices.astype(F32).T, mix.T], axis=0)
    info = lax.all_to_all(
        jnp.broadcast_to(info[None], (near, *info.shape)),
        "expert",
        split_axis=0,
        concat_axis=0,
        tiled=True,
        axis_index_groups=rings,
    )
    slot, weight = route(info, columns, top)
    weights = jnp.concatenate(gates + ups, axis=1)
    shared = jnp.stack([s.reshape(3, units, width) for s in small], axis=1)
    shared = shared.reshape(3, CORES, pieces * units // CORES, width)

    def side(which):
        numbers = which * half + jnp.arange(half, dtype=jnp.int32)
        picks = slot[:, None, :] == numbers[None, :, None]
        slot_weight = jnp.sum(jnp.where(picks, weight[:, None, :], 0.0), axis=2)
        rows = lax.dynamic_index_in_dim(shared, which, axis=1, keepdims=False)
        return picks.astype(BF), slot_weight, rows

    mine, other = side(core), side(1 - core)
    total = near * tok
    rows = near * half // chips
    down, everyone = lax.optimization_barrier((expert_down, everyone))
    downs = jnp.concatenate(with_mates(down), axis=0)

    def sums(picks, shared_rows):
        received = dot("nct,ntd->ncd", picks, everyone.reshape(near, tok, width)).astype(BF)
        routed = dot("jrd,dp->jrp", received.reshape(chips, rows, width), weights).astype(BF)
        wanted = shared_rows[:2].reshape(2, chips, -1, width).transpose(1, 0, 2, 3)
        units_of = dot("hd,td->ht", wanted.reshape(-1, width), everyone).astype(BF)
        units_of = units_of.reshape(chips, -1, total)
        if total != routed.shape[2]:
            units_of = units_of.reshape(chips, -1, routed.shape[2])
        return jnp.concatenate([routed, units_of], axis=1)

    theirs = lax.ppermute(sums(other[0], other[2]), "tensor", partner)
    both = (sums(mine[0], mine[2]).astype(F32) + theirs.astype(F32)).astype(BF)
    chip = lax.axis_index("tensor") // CORES
    summed = 0.0
    for shift in (*range(1, chips), 0):
        term = lax.dynamic_index_in_dim(both, (chip + shift) % chips, keepdims=False)
        if shift:
            hop = [(t, (t + CORES * shift) % parts) for t in range(parts)]
            term = lax.ppermute(term, "tensor", hop)
        summed = summed + term.astype(F32)
    routed = summed[:rows]
    pair = summed[rows:].reshape(2, -1, total)
    routed = (jax.nn.silu(routed[:, :FFE]) * routed[:, FFE:]).astype(BF)
    shared_hidden = (jax.nn.silu(pair[0]) * pair[1]).astype(BF).reshape(-1, FFE)
    hidden = jnp.concatenate([routed, shared_hidden], axis=0)
    hidden = lax.all_gather(hidden, "tensor", axis=0, axis_index_groups=crosses)
    their_hidden = lax.ppermute(hidden, "tensor", partner)

    def outs(hidden, slot_weight):
        out = dot("rp,pd->rd", hidden[:, :rows].reshape(near * half, FFE), downs)
        out = (out.reshape(near, half, width) * slot_weight[:, :, None]).astype(BF)
        units_of = hidden[:, rows:].reshape(-1, near, tok).transpose(1, 0, 2)
        return out, units_of

    (out_a, units_a), (out_b, units_b) = outs(hidden, mine[1]), outs(their_hidden, other[1])
    spread = [
        jnp.broadcast_to(s[2][2], (near, *s[2].shape[1:])) for s in (mine, other)
    ]
    share = dot(
        "nkt,nkd->ntd",
        jnp.concatenate([mine[0], other[0], units_a, units_b], axis=1),
        jnp.concatenate([out_a, out_b, *spread], axis=1),
    )
    return lax.psum_scatter(
        share.astype(BF).reshape(total, width),
        "expert",
        scatter_dimension=0,
        tiled=True,
        axis_index_groups=rings,
    )


def solution(mesh):
    placed = (
        P(("groups", "expert"), "tensor"),
        P(("groups", "expert"), None),
        P(("groups", "expert"), None),
        P("tensor", "expert"),
        P("tensor", "expert"),
        P("expert", "tensor"),
        P(None, "expert", "tensor"),
        P("expert", "tensor"),
    )

    return jax.shard_map(
        local,
        mesh=mesh,
        in_specs=placed,
        out_specs=P(("groups", "expert"), "tensor"),
        check_vma=False,
    )
```

profile of v0, /device:TPU:34, one launch (start us, length us, event | category | flops | bytes accessed | tf_op | source)
XLA Modules:
  0.0 378.1 jit_solution(36877141896545052)
XLA Ops:
  8.3 4.7 %collective-permute-start.2 = (bf16[96,896]{1,0:T(8,128)(2,1)S(1)}, bf16[96,896]{1,0:T(8,128)(2,1)S(1)}, u32[]{:S(2)}, u32[]{:S(2)}) collective-permute-start(bf16[96,896]{1,0:T(8,128)(2,1)S(1)} %pad_maximum_fusion.2), channel_id=1, source_target_pairs={{0,8},{8,0},{16,24},{24,16},{32,40},{40,32},{48,56},{56,48},{64,72... | collective-permute-start | bytes 516104 | tf_op jit(solution)/shard_map/ppermute | solution.py:48
  15.7 43.7 %all-to-all-start = ((f32[16,8,128]{2,1,0:T(8,128)}), f32[16,8,128]{2,1,0:T(8,128)S(1)}, u32[]{:S(2)}, u32[]{:S(2)}) async-start(f32[16,8,128]{2,1,0:T(8,128)} %broadcast_in_dim.47), calls=%async_computation | async-start | bytes 131072 | tf_op jit(solution)/shard_map/all_to_all | solution.py:62
  59.5 2.1 collective-permute-start
  61.6 3.8 %collective-permute-start.1 = (bf16[896,512]{1,0:T(8,128)(2,1)}, bf16[896,512]{1,0:T(8,128)(2,1)S(1)}, u32[]{:S(2)}, u32[]{:S(2)}) collective-permute-start(bf16[896,512]{1,0:T(8,128)(2,1)} %param.12), channel_id=1, source_target_pairs={{0,8},{8,0},{16,24},{24,16},{32,40},{40,32},{48,56},{56,48},{64,72... | collective-permute-start | bytes 2752520 | tf_op jit(solution)/shard_map/ppermute | solution.py:48
  65.7 21.4 %all-to-all-done = f32[16,8,128]{2,1,0:T(8,128)S(1)} async-done(((f32[16,8,128]{2,1,0:T(8,128)}), f32[16,8,128]{2,1,0:T(8,128)S(1)}, u32[]{:S(2)}, u32[]{:S(2)}) %all-to-all-start) | async-done | bytes 65568 | tf_op jit(solution)/shard_map/all_to_all | solution.py:62
  88.0 94.2 %all-gather.3.cloned.1.call-done = bf16[2048,896]{1,0:T(8,128)(2,1)} async-done(((bf16[128,896]{1,0:T(8,128)(2,1)}), bf16[2048,896]{1,0:T(8,128)(2,1)}) %all-gather.3.cloned.1.call-update) | async-done | bytes 3670032 | tf_op jit(solution)/shard_map/all_gather | solution.py:55
  182.2 3.4 convolution_convert_fusion.2
  186.4 2.9 convolution_convert_fusion
  189.6 2.0 collective-permute-start.3
  191.7 3.4 convolution_convert_fusion.3
  195.9 2.9 convolution_convert_fusion.1
  198.8 2.3 add_convert_fusion
  202.1 3.8 %collective-permute-start.4 = (bf16[112,2048]{1,0:T(8,128)(2,1)}, bf16[112,2048]{1,0:T(8,128)(2,1)S(1)}, u32[]{:S(2)}, u32[]{:S(2)}) collective-permute-start(bf16[112,2048]{1,0:T(8,128)(2,1)} %get-tuple-element.13), channel_id=1, source_target_pairs={{0,2},{1,3},{2,4},{3,5},{4,6},{5,7},{6,0},{7,1},{8,10},{9,11},{10,... | collective-permute-start | bytes 1376264 | tf_op jit(solution)/shard_map/ppermute | solution.py:106
  205.8 2.1 collective-permute-start.6
  208.0 4.4 %collective-permute-start.5 = (bf16[112,2048]{1,0:T(8,128)(2,1)S(1)}, bf16[112,2048]{1,0:T(8,128)(2,1)}, u32[]{:S(2)}, u32[]{:S(2)}) collective-permute-start(bf16[112,2048]{1,0:T(8,128)(2,1)S(1)} %get-tuple-element.15), channel_id=1, source_target_pairs={{0,4},{1,5},{2,6},{3,7},{4,0},{5,1},{6,2},{7,3},{8,12},{9,13},{10,... | collective-permute-start | bytes 1376264 | tf_op jit(solution)/shard_map/ppermute | solution.py:106
  212.4 2.0 collective-permute-start.8
  214.3 12.1 %collective-permute-done.4 = bf16[112,2048]{1,0:T(8,128)(2,1)S(1)} collective-permute-done((bf16[112,2048]{1,0:T(8,128)(2,1)}, bf16[112,2048]{1,0:T(8,128)(2,1)S(1)}, u32[]{:S(2)}, u32[]{:S(2)}) %collective-permute-start.4) | collective-permute-done | bytes 458784 | tf_op jit(solution)/shard_map/ppermute | solution.py:106
  226.5 4.4 %collective-permute-done.5 = bf16[112,2048]{1,0:T(8,128)(2,1)} collective-permute-done((bf16[112,2048]{1,0:T(8,128)(2,1)S(1)}, bf16[112,2048]{1,0:T(8,128)(2,1)}, u32[]{:S(2)}, u32[]{:S(2)}) %collective-permute-start.5) | collective-permute-done | bytes 458784 | tf_op jit(solution)/shard_map/ppermute | solution.py:106
  232.6 13.9 %all-gather = bf16[448,1024]{1,0:T(8,128)(2,1)S(1)} all-gather(bf16[112,1024]{1,0:T(8,128)(2,1)S(1)} %pad_maximum_fusion.1), channel_id=2, replica_groups={{0,2,4,6},{1,3,5,7},{8,10,12,14},{9,11,13,15},{16,18,20,22},{17,19,21,2..., dimensions={0}, use_global_device_ids=true | all-gather | bytes 1146880 | tf_op jit(solution)/shard_map/all_gather | solution.py:113
  246.4 2.1 collective-permute-start.7
  249.2 3.3 fusion.11
  252.7 2.5 fusion.12
  255.4 2.7 fusion.8
  258.2 113.1 %reduce-scatter.2.cloned.1.call-done = bf16[128,896]{1,0:T(8,128)(2,1)} async-done(((bf16[2048,896]{1,0:T(8,128)(2,1)}), bf16[128,896]{1,0:T(8,128)(2,1)}) %reduce-scatter.2.cloned.1.call-update) | async-done | bytes 229392 | tf_op jit(solution)/shard_map/reduce_scatter | solution.py:131
  (81 shorter events, 10.7 us)
Async XLA Ops:
  6.5 175.6 %all-gather.3.cloned.1.call-start = ((), (), s32[]{:S(2)}) async-start(), calls=%async_computation.2 | async-start | bytes 3899392 | tf_op jit(solution)/shard_map/all_gather | solution.py:55
  8.3 57.2 %collective-permute-start.2 = (bf16[96,896]{1,0:T(8,128)(2,1)S(1)}, bf16[96,896]{1,0:T(8,128)(2,1)S(1)}, u32[]{:S(2)}, u32[]{:S(2)}) collective-permute-start(bf16[96,896]{1,0:T(8,128)(2,1)S(1)} %pad_maximum_fusion.2), channel_id=1, source_target_pairs={{0,8},{8,0},{16,24},{24,16},{32,40},{40,32},{48,56},{56,48},{64,72... | collective-permute-start | bytes 516104 | tf_op jit(solution)/shard_map/ppermute | solution.py:48
  15.7 71.4 %all-to-all-start = ((f32[16,8,128]{2,1,0:T(8,128)}), f32[16,8,128]{2,1,0:T(8,128)S(1)}, u32[]{:S(2)}, u32[]{:S(2)}) async-start(f32[16,8,128]{2,1,0:T(8,128)} %broadcast_in_dim.47), calls=%async_computation | async-start | bytes 131072 | tf_op jit(solution)/shard_map/all_to_all | solution.py:62
  59.4 311.8 %reduce-scatter.2.cloned.1.call-start = ((), (), s32[]{:S(2)}) async-start(), calls=%async_computation.3 | async-start | bytes 3899392 | tf_op jit(solution)/shard_map/reduce_scatter | solution.py:131
  59.5 126.9 %collective-permute-start = (bf16[896,512]{1,0:T(8,128)(2,1)}, bf16[896,512]{1,0:T(8,128)(2,1)S(1)}, u32[]{:S(2)}, u32[]{:S(2)}) collective-permute-start(bf16[896,512]{1,0:T(8,128)(2,1)} %param.11), channel_id=1, source_target_pairs={{0,8},{8,0},{16,24},{24,16},{32,40},{40,32},{48,56},{56,48},{64,72... | collective-permute-start | bytes 2752520 | tf_op jit(solution)/shard_map/ppermute | solution.py:48
  61.6 124.8 %collective-permute-start.1 = (bf16[896,512]{1,0:T(8,128)(2,1)}, bf16[896,512]{1,0:T(8,128)(2,1)S(1)}, u32[]{:S(2)}, u32[]{:S(2)}) collective-permute-start(bf16[896,512]{1,0:T(8,128)(2,1)} %param.12), channel_id=1, source_target_pairs={{0,8},{8,0},{16,24},{24,16},{32,40},{40,32},{48,56},{56,48},{64,72... | collective-permute-start | bytes 2752520 | tf_op jit(solution)/shard_map/ppermute | solution.py:48
  65.5 120.9 %copy-start.5 = (s32[24]{0:T(128)}, s32[24]{0:T(128)S(1)}, u32[]{:S(2)}) copy-start(s32[24]{0:T(128)S(1)} %get-tuple-element.24) | copy-start | bytes 292
  65.5 129.6 %copy-start.7 = (s32[24]{0:T(128)}, s32[24]{0:T(128)S(1)}, u32[]{:S(2)}) copy-start(s32[24]{0:T(128)S(1)} %get-tuple-element.25) | copy-start | bytes 292
  88.0 107.2 %copy-start.2 = (s32[16,128]{1,0:T(8,128)}, s32[16,128]{1,0:T(8,128)S(1)}, u32[]{:S(2)}) copy-start(s32[16,128]{1,0:T(8,128)S(1)} %fusion.13) | copy-start | bytes 24580
  182.2 4.2 %copy-start.9 = (bf16[896,512]{1,0:T(8,128)(2,1)S(1)}, bf16[896,512]{1,0:T(8,128)(2,1)}, u32[]{:S(2)}) copy-start(bf16[896,512]{1,0:T(8,128)(2,1)} %param.12) | copy-start | bytes 2752516
  182.2 4.2 %copy-start.10 = (bf16[896,512]{1,0:T(8,128)(2,1)S(1)}, bf16[896,512]{1,0:T(8,128)(2,1)}, u32[]{:S(2)}) copy-start(bf16[896,512]{1,0:T(8,128)(2,1)} %param.11) | copy-start | bytes 2752516
  189.6 9.2 %collective-permute-start.3 = (bf16[4,112,2048]{2,1,0:T(8,128)(2,1)S(1)}, bf16[4,112,2048]{2,1,0:T(8,128)(2,1)}, u32[]{:S(2)}, u32[]{:S(2)}) collective-permute-start(bf16[4,112,2048]{2,1,0:T(8,128)(2,1)S(1)} %pad_maximum_fusion), channel_id=1, source_target_pairs={{0,1},{1,0},{2,3},{3,2},{4,5},{5,4},{6,7},{7,6},{8,9},{9,8},{10,11... | collective-permute-start | bytes 5505032 | tf_op jit(solution)/shard_map/ppermute | solution.py:98
  191.6 4.2 %copy-start.11 = (bf16[896,512]{1,0:T(8,128)(2,1)S(1)}, bf16[896,512]{1,0:T(8,128)(2,1)}, u32[]{:S(2)}) copy-start(bf16[896,512]{1,0:T(8,128)(2,1)} %param.11) | copy-start | bytes 2752516
  191.6 4.2 %copy-start.13 = (bf16[896,512]{1,0:T(8,128)(2,1)S(1)}, bf16[896,512]{1,0:T(8,128)(2,1)}, u32[]{:S(2)}) copy-start(bf16[896,512]{1,0:T(8,128)(2,1)} %copy-done.12) | copy-start | bytes 2752516
  191.7 4.2 %copy-start.15 = (bf16[896,512]{1,0:T(8,128)(2,1)S(1)}, bf16[896,512]{1,0:T(8,128)(2,1)}, u32[]{:S(2)}) copy-start(bf16[896,512]{1,0:T(8,128)(2,1)} %copy-done.14) | copy-start | bytes 2752516
  202.1 24.4 %collective-permute-start.4 = (bf16[112,2048]{1,0:T(8,128)(2,1)}, bf16[112,2048]{1,0:T(8,128)(2,1)S(1)}, u32[]{:S(2)}, u32[]{:S(2)}) collective-permute-start(bf16[112,2048]{1,0:T(8,128)(2,1)} %get-tuple-element.13), channel_id=1, source_target_pairs={{0,2},{1,3},{2,4},{3,5},{4,6},{5,7},{6,0},{7,1},{8,10},{9,11},{10,... | collective-permute-start | bytes 1376264 | tf_op jit(solution)/shard_map/ppermute | solution.py:106
  205.8 20.6 %collective-permute-start.6 = (bf16[112,2048]{1,0:T(8,128)(2,1)S(1)}, bf16[112,2048]{1,0:T(8,128)(2,1)}, u32[]{:S(2)}, u32[]{:S(2)}) collective-permute-start(bf16[112,2048]{1,0:T(8,128)(2,1)S(1)} %get-tuple-element.14), channel_id=1, source_target_pairs={{0,6},{1,7},{2,0},{3,1},{4,2},{5,3},{6,4},{7,5},{8,14},{9,15},{10,... | collective-permute-start | bytes 1376264 | tf_op jit(solution)/shard_map/ppermute | solution.py:106
  208.0 22.9 %collective-permute-start.5 = (bf16[112,2048]{1,0:T(8,128)(2,1)S(1)}, bf16[112,2048]{1,0:T(8,128)(2,1)}, u32[]{:S(2)}, u32[]{:S(2)}) collective-permute-start(bf16[112,2048]{1,0:T(8,128)(2,1)S(1)} %get-tuple-element.15), channel_id=1, source_target_pairs={{0,4},{1,5},{2,6},{3,7},{4,0},{5,1},{6,2},{7,3},{8,12},{9,13},{10,... | collective-permute-start | bytes 1376264 | tf_op jit(solution)/shard_map/ppermute | solution.py:106
  212.4 36.8 %collective-permute-start.8 = (bf16[512,896]{1,0:T(8,128)(2,1)}, bf16[512,896]{1,0:T(8,128)(2,1)}, u32[]{:S(2)}, u32[]{:S(2)}) collective-permute-start(bf16[512,896]{1,0:T(8,128)(2,1)} %param.13), channel_id=1, source_target_pairs={{0,8},{8,0},{16,24},{24,16},{32,40},{40,32},{48,56},{56,48},{64,72... | collective-permute-start | bytes 2752520 | tf_op jit(solution)/shard_map/ppermute | solution.py:48
  226.4 22.2 %copy-start.3 = (s32[16,128]{1,0:T(8,128)S(1)}, s32[16,128]{1,0:T(8,128)}, u32[]{:S(2)}) copy-start(s32[16,128]{1,0:T(8,128)} %copy-done.2) | copy-start | bytes 24580
  226.4 22.2 %copy-start.4 = (f32[16,128]{1,0:T(8,128)S(1)}, f32[16,128]{1,0:T(8,128)}, u32[]{:S(2)}) copy-start(f32[16,128]{1,0:T(8,128)} %get-tuple-element.11) | copy-start | bytes 24580
  226.4 22.2 %copy-start.6 = (s32[24]{0:T(128)S(1)}, s32[24]{0:T(128)}, u32[]{:S(2)}) copy-start(s32[24]{0:T(128)} %copy-done.5) | copy-start | bytes 292
  226.4 22.2 %copy-start.8 = (s32[24]{0:T(128)S(1)}, s32[24]{0:T(128)}, u32[]{:S(2)}) copy-start(s32[24]{0:T(128)} %copy-done.7) | copy-start | bytes 292
  246.4 6.1 %collective-permute-start.7 = (bf16[4,112,1024]{2,1,0:T(8,128)(2,1)S(1)}, bf16[4,112,1024]{2,1,0:T(8,128)(2,1)S(1)}, u32[]{:S(2)}, u32[]{:S(2)}) collective-permute-start(bf16[4,112,1024]{2,1,0:T(8,128)(2,1)S(1)} %bitcast.67), channel_id=1, source_target_pairs={{0,1},{1,0},{2,3},{3,2},{4,5},{5,4},{6,7},{7,6},{8,9},{9,8},{10,11... | collective-permute-start | bytes 2752520 | tf_op jit(solution)/shard_map/ppermute | solution.py:114
  (5 other events, 15.6 us)
Sparse Core Ops, SparseCore 0:
  9.4 172.7 all-gather.2
  258.3 112.9 reduce-scatter.1
where the time goes:
time: 379 us; the launch traced here: 378 us
  waiting for transfers between devices  246 us (65%)
  starting transfers between devices  70.7 us (19%)
  matrix products  22.8 us (6%)
  between operations  14.1 us (4%)
  blocking collectives  13.9 us (4%)
  other arithmetic  8.31 us (2%)
    reduce_scatter x1, waiting for transfers between devices, local(): lax.psum_scatter(share.astype(BF).reshape(total, width), 'expert', scatte...  113 us
    all_gather x1, waiting for transfers between devices, local(): lax.all_gather(tokens, 'expert', axis=0, tiled=True, axis_index_groups=ri...  94.2 us
    all_to_all x1, starting transfers between devices, local(): lax.all_to_all(jnp.broadcast_to(info[None], (near, *info.shape)), 'expert...  43.7 us
    dot_general x10, matrix products, dot(): return jnp.einsum(spec, a, b, preferred_element_type=F32)  22.8 us
    all_to_all x1, waiting for transfers between devices, local(): lax.all_to_all(jnp.broadcast_to(info[None], (near, *info.shape)), 'expert...  21.4 us
    ppermute x3, waiting for transfers between devices, local(): term = lax.ppermute(term, 'tensor', hop)  16.6 us
    all_gather x1, blocking collectives, local(): hidden = lax.all_gather(hidden, 'tensor', axis=0, axis_index_groups=crosses)  13.9 us
    ppermute x4, starting transfers between devices, with_mates(): lax.ppermute(array, 'expert', [(z, z - z % pieces + (z + shift) % pieces)...  12.6 us
  transfers between devices with their start and end apart: 12, of which 5 were waited for; matrix products, arithmetic and copies ran while one was open for 6% of the time, Pallas kernels for 0%

commit v1 on v0

--- a/solution.py
+++ b/solution.py
@@ -54,8 +54,8 @@
 
     everyone = lax.all_gather(tokens, "expert", axis=0, tiled=True, axis_index_groups=rings)
     gates = with_mates(expert_gate)
-    ups = with_mates(expert_up)
-    small = with_mates(jnp.concatenate([shared_in.reshape(2 * units, width), shared_down], axis=0))
+    small = jnp.concatenate([shared_in.reshape(2 * units, width), shared_down], axis=0)
+    small = with_mates(small)
     sigmoids = jax.nn.sigmoid(affinity)
     mix = 2.5 * sigmoids / jnp.sum(sigmoids, axis=1, keepdims=True)
     info = jnp.concatenate([choices.astype(F32).T, mix.T], axis=0)
@@ -68,7 +68,6 @@
         axis_index_groups=rings,
     )
     slot, weight = route(info, columns, top)
-    weights = jnp.concatenate(gates + ups, axis=1)
     shared = jnp.stack([s.reshape(3, units, width) for s in small], axis=1)
     shared = shared.reshape(3, CORES, pieces * units // CORES, width)
 
@@ -82,32 +81,48 @@
     mine, other = side(core), side(1 - core)
     total = near * tok
     rows = near * half // chips
-    down, everyone = lax.optimization_barrier((expert_down, everyone))
+    late_up, down, everyone = lax.optimization_barrier((expert_up, expert_down, everyone))
+    ups = with_mates(late_up)
     downs = jnp.concatenate(with_mates(down), axis=0)
+    received = [
+        dot("nct,ntd->ncd", picks, everyone.reshape(near, tok, width))
+        .astype(BF)
+        .reshape(chips, rows, width)
+        for picks, _, _ in (mine, other)
+    ]
+    chip = lax.axis_index("tensor") // CORES
 
-    def sums(picks, shared_rows):
-        received = dot("nct,ntd->ncd", picks, everyone.reshape(near, tok, width)).astype(BF)
-        routed = dot("jrd,dp->jrp", received.reshape(chips, rows, width), weights).astype(BF)
+    def first(which):
+        weights = jnp.concatenate([*gates, expert_up], axis=1)
+        return dot("jrd,dp->jrp", received[which], weights).astype(BF)
+
+    def second(which):
+        late = [dot("jrd,dp->jrp", received[which], up).astype(BF) for up in ups[1:]]
+        shared_rows = (mine, other)[which][2]
         wanted = shared_rows[:2].reshape(2, chips, -1, width).transpose(1, 0, 2, 3)
         units_of = dot("hd,td->ht", wanted.reshape(-1, width), everyone).astype(BF)
-        units_of = units_of.reshape(chips, -1, total)
-        if total != routed.shape[2]:
-            units_of = units_of.reshape(chips, -1, routed.shape[2])
-        return jnp.concatenate([routed, units_of], axis=1)
+        return jnp.concatenate([*late, units_of.reshape(chips, -1, columns)], axis=1)
 
-    theirs = lax.ppermute(sums(other[0], other[2]), "tensor", partner)
-    both = (sums(mine[0], mine[2]).astype(F32) + theirs.astype(F32)).astype(BF)
-    chip = lax.axis_index("tensor") // CORES
-    summed = 0.0
-    for shift in (*range(1, chips), 0):
-        term = lax.dynamic_index_in_dim(both, (chip + shift) % chips, keepdims=False)
-        if shift:
+    def summed(partials):
+        theirs = lax.ppermute(partials(1), "tensor", partner)
+        both = (partials(0).astype(F32) + theirs.astype(F32)).astype(BF)
+        total_of = lax.dynamic_index_in_dim(both, chip, keepdims=False).astype(F32)
+        for shift in range(1, chips):
+            term = lax.dynamic_index_in_dim(both, (chip + shift) % chips, keepdims=False)
             hop = [(t, (t + CORES * shift) % parts) for t in range(parts)]
             term = lax.ppermute(term, "tensor", hop)
-        summed = summed + term.astype(F32)
-    routed = summed[:rows]
-    pair = summed[rows:].reshape(2, -1, total)
-    routed = (jax.nn.silu(routed[:, :FFE]) * routed[:, FFE:]).astype(BF)
+            total_of = total_of + term.astype(F32)
+        return total_of
+
+    early, late = summed(first), summed(second)
+    gate_of, up_of = early[:, :FFE], [early[:, FFE:]]
+    up_of += [late[rows * p : rows * (p + 1)] for p in range(pieces - 1)]
+    pair = late[rows * (pieces - 1) :].reshape(2, -1, total)
+    routed = [
+        (jax.nn.silu(gate_of[:, columns * p : columns * (p + 1)]) * up_of[p]).astype(BF)
+        for p in range(pieces)
+    ]
+    routed = jnp.concatenate(routed, axis=1)
     shared_hidden = (jax.nn.silu(pair[0]) * pair[1]).astype(BF).reshape(-1, FFE)
     hidden = jnp.concatenate([routed, shared_hidden], axis=0)
     hidden = lax.all_gather(hidden, "tensor", axis=0, axis_index_groups=crosses)

time: 379 us -> 383 us (1.011)
  the two profiles are of different devices: /device:TPU:34 before, /device:TPU:38 now
where the time goes in v1:
time: 383 us; the launch traced here: 382 us
  waiting for transfers between devices  238 us (62%)
  starting transfers between devices  81.8 us (21%)
  matrix products  28.7 us (7%)
  between operations  14.1 us (4%)
  blocking collectives  13.6 us (4%)
  other arithmetic  4.27 us (1%)
    reduce_scatter x1, waiting for transfers between devices, local(): lax.psum_scatter(share.astype(BF).reshape(total, width), 'expert', scatte...  110 us
    all_gather x1, waiting for transfers between devices, local(): lax.all_gather(tokens, 'expert', axis=0, tiled=True, axis_index_groups=ri...  83.5 us
    all_to_all x1, starting transfers between devices, local(): lax.all_to_all(jnp.broadcast_to(info[None], (near, *info.shape)), 'expert...  43.7 us
    dot_general x12, matrix products, dot(): return jnp.einsum(spec, a, b, preferred_element_type=F32)  28.7 us
    all_to_all x1, waiting for transfers between devices, local(): lax.all_to_all(jnp.broadcast_to(info[None], (near, *info.shape)), 'expert...  25.1 us
    ppermute x6, starting transfers between devices, summed(): term = lax.ppermute(term, 'tensor', hop)  19.2 us
    ppermute x6, waiting for transfers between devices, summed(): term = lax.ppermute(term, 'tensor', hop)  13.9 us
    all_gather x1, blocking collectives, local(): hidden = lax.all_gather(hidden, 'tensor', axis=0, axis_index_groups=crosses)  13.6 us
  transfers between devices with their start and end apart: 16, of which 7 were waited for; matrix products, arithmetic and copies ran while one was open for 8% of the time, Pallas kernels for 0%

profile of v1, /device:TPU:38, one launch (start us, length us, event | category | flops | bytes accessed | tf_op | source)
XLA Modules:
  0.0 382.1 jit_solution(8767792578314160182)
XLA Ops:
  8.3 4.7 %collective-permute-start.6 = (bf16[96,896]{1,0:T(8,128)(2,1)S(1)}, bf16[96,896]{1,0:T(8,128)(2,1)S(1)}, u32[]{:S(2)}, u32[]{:S(2)}) collective-permute-start(bf16[96,896]{1,0:T(8,128)(2,1)S(1)} %pad_maximum_fusion.2), channel_id=1, source_target_pairs={{0,8},{8,0},{16,24},{24,16},{32,40},{40,32},{48,56},{56,48},{64,72... | collective-permute-start | bytes 516104 | tf_op jit(solution)/shard_map/ppermute | solution.py:48
  15.7 43.7 %all-to-all-start = ((f32[16,8,128]{2,1,0:T(8,128)}), f32[16,8,128]{2,1,0:T(8,128)S(1)}, u32[]{:S(2)}, u32[]{:S(2)}) async-start(f32[16,8,128]{2,1,0:T(8,128)} %broadcast_in_dim.47), calls=%async_computation | async-start | bytes 131072 | tf_op jit(solution)/shard_map/all_to_all | solution.py:62
  59.5 2.1 collective-permute-start
  62.0 25.1 %all-to-all-done = f32[16,8,128]{2,1,0:T(8,128)S(1)} async-done(((f32[16,8,128]{2,1,0:T(8,128)}), f32[16,8,128]{2,1,0:T(8,128)S(1)}, u32[]{:S(2)}, u32[]{:S(2)}) %all-to-all-start) | async-done | bytes 65568 | tf_op jit(solution)/shard_map/all_to_all | solution.py:62
  87.3 83.5 %all-gather.3.cloned.1.call-done = bf16[2048,896]{1,0:T(8,128)(2,1)} async-done(((bf16[128,896]{1,0:T(8,128)(2,1)}), bf16[2048,896]{1,0:T(8,128)(2,1)}) %all-gather.3.cloned.1.call-update) | async-done | bytes 3670032 | tf_op jit(solution)/shard_map/all_gather | solution.py:55
  170.8 3.3 convolution_convert_fusion.3
  174.3 2.1 collective-permute-start.5
  176.4 2.7 convolution_convert_fusion.4
  179.2 4.0 %convolution_convert_fusion = bf16[4,96,1536]{2,1,0:T(8,128)(2,1)} fusion(bf16[4,96,896]{2,1,0:T(8,128)(2,1)S(1)} %bitcast.86, bf16[896,512]{1,0:T(8,128)(2,1)} %param.12, bf16[896,512]{1,0:T(8,128)(2,1)S(1)} %collective-permute-done, bf16[896,512]{1,0:T(8,128)(2,1)S(1)} %copy-done.1), kind=kOutput, calls=%fused_computation.8 | convolution fusion | flops 1065811968 | bytes 4620288 | tf_op jit(solution)/shard_map/jrd,dp->jrp/dot_general | solution.py:15
  186.5 4.0 %collective-permute-start.12 = (bf16[512,896]{1,0:T(8,128)(2,1)}, bf16[512,896]{1,0:T(8,128)(2,1)}, u32[]{:S(2)}, u32[]{:S(2)}) collective-permute-start(bf16[512,896]{1,0:T(8,128)(2,1)} %param.13), channel_id=1, source_target_pairs={{0,8},{8,0},{16,24},{24,16},{32,40},{40,32},{48,56},{56,48},{64,72... | collective-permute-start | bytes 2752520 | tf_op jit(solution)/shard_map/ppermute | solution.py:48
  190.5 2.7 convolution_convert_fusion.5
  193.2 4.6 %collective-permute-done.5 = bf16[896,512]{1,0:T(8,128)(2,1)} collective-permute-done((bf16[896,512]{1,0:T(8,128)(2,1)}, bf16[896,512]{1,0:T(8,128)(2,1)}, u32[]{:S(2)}, u32[]{:S(2)}) %collective-permute-start.5) | collective-permute-done | bytes 917536 | tf_op jit(solution)/shard_map/ppermute | solution.py:48
  203.4 2.6 fusion.10
  206.1 5.3 %collective-permute-start.2 = (bf16[96,1536]{1,0:T(8,128)(2,1)S(1)}, bf16[96,1536]{1,0:T(8,128)(2,1)S(1)}, u32[]{:S(2)}, u32[]{:S(2)}) collective-permute-start(bf16[96,1536]{1,0:T(8,128)(2,1)S(1)} %get-tuple-element.15), channel_id=1, source_target_pairs={{0,2},{1,3},{2,4},{3,5},{4,6},{5,7},{6,0},{7,1},{8,10},{9,11},{10,... | collective-permute-start | bytes 884744 | tf_op jit(solution)/shard_map/ppermute | solution.py:113
  213.3 3.5 collective-permute-start.3
  217.1 4.6 %collective-permute-start.8 = (bf16[160,512]{1,0:T(8,128)(2,1)S(1)}, bf16[160,512]{1,0:T(8,128)(2,1)S(1)}, u32[]{:S(2)}, u32[]{:S(2)}) collective-permute-start(bf16[160,512]{1,0:T(8,128)(2,1)S(1)} %get-tuple-element.18), channel_id=1, source_target_pairs={{0,2},{1,3},{2,4},{3,5},{4,6},{5,7},{6,0},{7,1},{8,10},{9,11},{10,... | collective-permute-start | bytes 491528 | tf_op jit(solution)/shard_map/ppermute | solution.py:113
  223.6 7.1 %collective-permute-done.4 = bf16[96,1536]{1,0:T(8,128)(2,1)S(1)} collective-permute-done((bf16[96,1536]{1,0:T(8,128)(2,1)S(1)}, bf16[96,1536]{1,0:T(8,128)(2,1)S(1)}, u32[]{:S(2)}, u32[]{:S(2)}) %collective-permute-start.4) | collective-permute-done | bytes 294944 | tf_op jit(solution)/shard_map/ppermute | solution.py:113
  233.4 6.2 %collective-permute-done.9 = bf16[160,512]{1,0:T(8,128)(2,1)S(1)} collective-permute-done((bf16[160,512]{1,0:T(8,128)(2,1)S(1)}, bf16[160,512]{1,0:T(8,128)(2,1)S(1)}, u32[]{:S(2)}, u32[]{:S(2)}) %collective-permute-start.9) | collective-permute-done | bytes 163872 | tf_op jit(solution)/shard_map/ppermute | solution.py:113
  240.0 13.6 %all-gather = bf16[448,1024]{1,0:T(8,128)(2,1)S(1)} all-gather(bf16[112,1024]{1,0:T(8,128)(2,1)S(1)} %pad_maximum_fusion.1), channel_id=2, replica_groups={{0,2,4,6},{1,3,5,7},{8,10,12,14},{9,11,13,15},{16,18,20,22},{17,19,21,2..., dimensions={0}, use_global_device_ids=true | all-gather | bytes 1146880 | tf_op jit(solution)/shard_map/all_gather | solution.py:128
  253.6 2.1 collective-permute-start.11
  256.3 3.3 fusion.14
  259.9 2.5 fusion.15
  262.6 2.6 fusion.11
  265.3 110.0 %reduce-scatter.2.cloned.1.call-done = bf16[128,896]{1,0:T(8,128)(2,1)} async-done(((bf16[2048,896]{1,0:T(8,128)(2,1)}), bf16[128,896]{1,0:T(8,128)(2,1)}) %reduce-scatter.2.cloned.1.call-update) | async-done | bytes 229392 | tf_op jit(solution)/shard_map/reduce_scatter | solution.py:146
  (75 shorter events, 22.1 us)
Async XLA Ops:
  6.5 164.3 %all-gather.3.cloned.1.call-start = ((), (), s32[]{:S(2)}) async-start(), calls=%async_computation.2 | async-start | bytes 3899392 | tf_op jit(solution)/shard_map/all_gather | solution.py:55
  8.3 53.4 %collective-permute-start.6 = (bf16[96,896]{1,0:T(8,128)(2,1)S(1)}, bf16[96,896]{1,0:T(8,128)(2,1)S(1)}, u32[]{:S(2)}, u32[]{:S(2)}) collective-permute-start(bf16[96,896]{1,0:T(8,128)(2,1)S(1)} %pad_maximum_fusion.2), channel_id=1, source_target_pairs={{0,8},{8,0},{16,24},{24,16},{32,40},{40,32},{48,56},{56,48},{64,72... | collective-permute-start | bytes 516104 | tf_op jit(solution)/shard_map/ppermute | solution.py:48
  15.7 71.4 %all-to-all-start = ((f32[16,8,128]{2,1,0:T(8,128)}), f32[16,8,128]{2,1,0:T(8,128)S(1)}, u32[]{:S(2)}, u32[]{:S(2)}) async-start(f32[16,8,128]{2,1,0:T(8,128)} %broadcast_in_dim.47), calls=%async_computation | async-start | bytes 131072 | tf_op jit(solution)/shard_map/all_to_all | solution.py:62
  59.4 315.8 %reduce-scatter.2.cloned.1.call-start = ((), (), s32[]{:S(2)}) async-start(), calls=%async_computation.3 | async-start | bytes 3899392 | tf_op jit(solution)/shard_map/reduce_scatter | solution.py:146
  59.5 119.6 %collective-permute-start = (bf16[896,512]{1,0:T(8,128)(2,1)}, bf16[896,512]{1,0:T(8,128)(2,1)S(1)}, u32[]{:S(2)}, u32[]{:S(2)}) collective-permute-start(bf16[896,512]{1,0:T(8,128)(2,1)} %param.11), channel_id=1, source_target_pairs={{0,8},{8,0},{16,24},{24,16},{32,40},{40,32},{48,56},{56,48},{64,72... | collective-permute-start | bytes 2752520 | tf_op jit(solution)/shard_map/ppermute | solution.py:48
  174.1 5.1 %copy-start.1 = (bf16[896,512]{1,0:T(8,128)(2,1)S(1)}, bf16[896,512]{1,0:T(8,128)(2,1)}, u32[]{:S(2)}) copy-start(bf16[896,512]{1,0:T(8,128)(2,1)} %param.11) | copy-start | bytes 2752516
  174.3 23.6 %collective-permute-start.5 = (bf16[896,512]{1,0:T(8,128)(2,1)}, bf16[896,512]{1,0:T(8,128)(2,1)}, u32[]{:S(2)}, u32[]{:S(2)}) collective-permute-start(bf16[896,512]{1,0:T(8,128)(2,1)} %param.12), channel_id=1, source_target_pairs={{0,8},{8,0},{16,24},{24,16},{32,40},{40,32},{48,56},{56,48},{64,72... | collective-permute-start | bytes 2752520 | tf_op jit(solution)/shard_map/ppermute | solution.py:48
  179.1 4.0 %copy-start.3 = (bf16[896,512]{1,0:T(8,128)(2,1)}, bf16[896,512]{1,0:T(8,128)(2,1)S(1)}, u32[]{:S(2)}) copy-start(bf16[896,512]{1,0:T(8,128)(2,1)S(1)} %collective-permute-done) | copy-start | bytes 2752516
  179.1 5.9 %copy-start = (bf16[2048,896]{1,0:T(8,128)(2,1)S(1)}, bf16[2048,896]{1,0:T(8,128)(2,1)}, u32[]{:S(2)}) copy-start(bf16[2048,896]{1,0:T(8,128)(2,1)} %all-gather.3.cloned.1.call-done) | copy-start | bytes 11010052
  183.1 20.2 %collective-permute-start.1 = (bf16[4,96,1536]{2,1,0:T(8,128)(2,1)}, bf16[4,96,1536]{2,1,0:T(8,128)(2,1)S(1)}, u32[]{:S(2)}, u32[]{:S(2)}) collective-permute-start(bf16[4,96,1536]{2,1,0:T(8,128)(2,1)} %convolution_convert_fusion), channel_id=1, source_target_pairs={{0,1},{1,0},{2,3},{3,2},{4,5},{5,4},{6,7},{7,6},{8,9},{9,8},{10,11... | collective-permute-start | bytes 3538952 | tf_op jit(solution)/shard_map/ppermute | solution.py:107
  186.5 69.8 %collective-permute-start.12 = (bf16[512,896]{1,0:T(8,128)(2,1)}, bf16[512,896]{1,0:T(8,128)(2,1)}, u32[]{:S(2)}, u32[]{:S(2)}) collective-permute-start(bf16[512,896]{1,0:T(8,128)(2,1)} %param.13), channel_id=1, source_target_pairs={{0,8},{8,0},{16,24},{24,16},{32,40},{40,32},{48,56},{56,48},{64,72... | collective-permute-start | bytes 2752520 | tf_op jit(solution)/shard_map/ppermute | solution.py:48
  193.2 10.2 %copy-start.2 = (bf16[896,512]{1,0:T(8,128)(2,1)S(1)}, bf16[896,512]{1,0:T(8,128)(2,1)}, u32[]{:S(2)}) copy-start(bf16[896,512]{1,0:T(8,128)(2,1)} %param.11) | copy-start | bytes 2752516
  193.2 10.2 %copy-start.4 = (bf16[896,512]{1,0:T(8,128)(2,1)S(1)}, bf16[896,512]{1,0:T(8,128)(2,1)}, u32[]{:S(2)}) copy-start(bf16[896,512]{1,0:T(8,128)(2,1)} %copy-done.3) | copy-start | bytes 2752516
  199.6 17.2 %collective-permute-start.7 = (bf16[4,160,512]{2,1,0:T(8,128)(2,1)S(1)}, bf16[4,160,512]{2,1,0:T(8,128)(2,1)S(1)}, u32[]{:S(2)}, u32[]{:S(2)}) collective-permute-start(bf16[4,160,512]{2,1,0:T(8,128)(2,1)S(1)} %pad_maximum_fusion), channel_id=1, source_target_pairs={{0,1},{1,0},{2,3},{3,2},{4,5},{5,4},{6,7},{7,6},{8,9},{9,8},{10,11... | collective-permute-start | bytes 1966088 | tf_op jit(solution)/shard_map/ppermute | solution.py:107
  206.1 15.6 %collective-permute-start.2 = (bf16[96,1536]{1,0:T(8,128)(2,1)S(1)}, bf16[96,1536]{1,0:T(8,128)(2,1)S(1)}, u32[]{:S(2)}, u32[]{:S(2)}) collective-permute-start(bf16[96,1536]{1,0:T(8,128)(2,1)S(1)} %get-tuple-element.15), channel_id=1, source_target_pairs={{0,2},{1,3},{2,4},{3,5},{4,6},{5,7},{6,0},{7,1},{8,10},{9,11},{10,... | collective-permute-start | bytes 884744 | tf_op jit(solution)/shard_map/ppermute | solution.py:113
  211.3 19.3 %collective-permute-start.4 = (bf16[96,1536]{1,0:T(8,128)(2,1)S(1)}, bf16[96,1536]{1,0:T(8,128)(2,1)S(1)}, u32[]{:S(2)}, u32[]{:S(2)}) collective-permute-start(bf16[96,1536]{1,0:T(8,128)(2,1)S(1)} %get-tuple-element.16), channel_id=1, source_target_pairs={{0,6},{1,7},{2,0},{3,1},{4,2},{5,3},{6,4},{7,5},{8,14},{9,15},{10,... | collective-permute-start | bytes 884744 | tf_op jit(solution)/shard_map/ppermute | solution.py:113
  213.3 19.3 %collective-permute-start.3 = (bf16[96,1536]{1,0:T(8,128)(2,1)S(1)}, bf16[96,1536]{1,0:T(8,128)(2,1)S(1)}, u32[]{:S(2)}, u32[]{:S(2)}) collective-permute-start(bf16[96,1536]{1,0:T(8,128)(2,1)S(1)} %get-tuple-element.17), channel_id=1, source_target_pairs={{0,4},{1,5},{2,6},{3,7},{4,0},{5,1},{6,2},{7,3},{8,12},{9,13},{10,... | collective-permute-start | bytes 884744 | tf_op jit(solution)/shard_map/ppermute | solution.py:113
  217.1 15.7 %collective-permute-start.8 = (bf16[160,512]{1,0:T(8,128)(2,1)S(1)}, bf16[160,512]{1,0:T(8,128)(2,1)S(1)}, u32[]{:S(2)}, u32[]{:S(2)}) collective-permute-start(bf16[160,512]{1,0:T(8,128)(2,1)S(1)} %get-tuple-element.18), channel_id=1, source_target_pairs={{0,2},{1,3},{2,4},{3,5},{4,6},{5,7},{6,0},{7,1},{8,10},{9,11},{10,... | collective-permute-start | bytes 491528 | tf_op jit(solution)/shard_map/ppermute | solution.py:113
  221.6 11.8 %collective-permute-start.10 = (bf16[160,512]{1,0:T(8,128)(2,1)S(1)}, bf16[160,512]{1,0:T(8,128)(2,1)S(1)}, u32[]{:S(2)}, u32[]{:S(2)}) collective-permute-start(bf16[160,512]{1,0:T(8,128)(2,1)S(1)} %get-tuple-element.19), channel_id=1, source_target_pairs={{0,6},{1,7},{2,0},{3,1},{4,2},{5,3},{6,4},{7,5},{8,14},{9,15},{10,... | collective-permute-start | bytes 491528 | tf_op jit(solution)/shard_map/ppermute | solution.py:113
  230.7 9.0 %collective-permute-start.9 = (bf16[160,512]{1,0:T(8,128)(2,1)S(1)}, bf16[160,512]{1,0:T(8,128)(2,1)S(1)}, u32[]{:S(2)}, u32[]{:S(2)}) collective-permute-start(bf16[160,512]{1,0:T(8,128)(2,1)S(1)} %get-tuple-element.20), channel_id=1, source_target_pairs={{0,4},{1,5},{2,6},{3,7},{4,0},{5,1},{6,2},{7,3},{8,12},{9,13},{10,... | collective-permute-start | bytes 491528 | tf_op jit(solution)/shard_map/ppermute | solution.py:113
  253.6 6.1 %collective-permute-start.11 = (bf16[4,112,1024]{2,1,0:T(8,128)(2,1)S(1)}, bf16[4,112,1024]{2,1,0:T(8,128)(2,1)S(1)}, u32[]{:S(2)}, u32[]{:S(2)}) collective-permute-start(bf16[4,112,1024]{2,1,0:T(8,128)(2,1)S(1)} %bitcast.81), channel_id=1, source_target_pairs={{0,1},{1,0},{2,3},{3,2},{4,5},{5,4},{6,7},{7,6},{8,9},{9,8},{10,11... | collective-permute-start | bytes 2752520 | tf_op jit(solution)/shard_map/ppermute | solution.py:129
  259.9 2.7 copy-start.5
Sparse Core Ops, SparseCore 0:
  9.4 161.3 all-gather.2
  265.4 109.7 reduce-scatter.1

commit v2 on v1

--- a/solution.py
+++ b/solution.py
@@ -90,7 +90,10 @@
         .reshape(chips, rows, width)
         for picks, _, _ in (mine, other)
     ]
-    chip = lax.axis_index("tensor") // CORES
+    wanted = jnp.stack([side_of[2][:2] for side_of in (mine, other)])
+    wanted = wanted.reshape(CORES, 2, chips, -1, width).transpose(0, 2, 1, 3, 4)
+    shared_sums = dot("hd,td->ht", wanted.reshape(-1, width), everyone).astype(BF)
+    shared_sums = shared_sums.reshape(CORES, chips, -1, columns)
 
     def first(which):
         weights = jnp.concatenate([*gates, expert_up], axis=1)
@@ -98,21 +101,15 @@
 
     def second(which):
         late = [dot("jrd,dp->jrp", received[which], up).astype(BF) for up in ups[1:]]
-        shared_rows = (mine, other)[which][2]
-        wanted = shared_rows[:2].reshape(2, chips, -1, width).transpose(1, 0, 2, 3)
-        units_of = dot("hd,td->ht", wanted.reshape(-1, width), everyone).astype(BF)
-        return jnp.concatenate([*late, units_of.reshape(chips, -1, columns)], axis=1)
+        return jnp.concatenate([*late, shared_sums[which]], axis=1)
 
     def summed(partials):
         theirs = lax.ppermute(partials(1), "tensor", partner)
         both = (partials(0).astype(F32) + theirs.astype(F32)).astype(BF)
-        total_of = lax.dynamic_index_in_dim(both, chip, keepdims=False).astype(F32)
-        for shift in range(1, chips):
-            term = lax.dynamic_index_in_dim(both, (chip + shift) % chips, keepdims=False)
-            hop = [(t, (t + CORES * shift) % parts) for t in range(parts)]
-            term = lax.ppermute(term, "tensor", hop)
-            total_of = total_of + term.astype(F32)
-        return total_of
+        crossed = lax.all_to_all(
+            both, "tensor", split_axis=0, concat_axis=0, tiled=True, axis_index_groups=crosses
+        )
+        return jnp.sum(crossed.astype(F32), axis=0)
 
     early, late = summed(first), summed(second)
     gate_of, up_of = early[:, :FFE], [early[:, FFE:]]

time: 383 us -> 383 us (level)
  the two profiles are of different devices: /device:TPU:38 before, /device:TPU:34 now
where the time goes in v2:
time: 383 us; the launch traced here: 382 us
  waiting for transfers between devices  247 us (64%)
  starting transfers between devices  72.5 us (19%)
  matrix products  28.9 us (8%)
  blocking collectives  13.9 us (4%)
  between operations  13.9 us (4%)
  other arithmetic  5.16 us (1%)
    reduce_scatter x1, waiting for transfers between devices, local(): lax.psum_scatter(share.astype(BF).reshape(total, width), 'expert', scatte...  112 us
    all_gather x1, waiting for transfers between devices, local(): lax.all_gather(tokens, 'expert', axis=0, tiled=True, axis_index_groups=ri...  83.9 us
    all_to_all x1, starting transfers between devices, local(): lax.all_to_all(jnp.broadcast_to(info[None], (near, *info.shape)), 'expert...  43.7 us
    dot_general x11, matrix products, dot(): return jnp.einsum(spec, a, b, preferred_element_type=F32)  28.9 us
    all_to_all x1, waiting for transfers between devices, local(): lax.all_to_all(jnp.broadcast_to(info[None], (near, *info.shape)), 'expert...  25.3 us
    all_to_all x2, waiting for transfers between devices, summed(): lax.all_to_all(both, 'tensor', split_axis=0, concat_axis=0, tiled=True, a...  18.3 us
    all_gather x1, blocking collectives, local(): hidden = lax.all_gather(hidden, 'tensor', axis=0, axis_index_groups=crosses)  13.9 us
    all_to_all x2, starting transfers between devices, summed(): lax.all_to_all(both, 'tensor', split_axis=0, concat_axis=0, tiled=True, a...  12 us
  transfers between devices with their start and end apart: 12, of which 6 were waited for; matrix products, arithmetic and copies ran while one was open for 8% of the time, Pallas kernels for 0%

profile of v2, /device:TPU:34, one launch (start us, length us, event | category | flops | bytes accessed | tf_op | source)
XLA Modules:
  0.0 382.4 jit_solution(16885182778931274857)
XLA Ops:
  8.3 4.7 %collective-permute-start.3 = (bf16[96,896]{1,0:T(8,128)(2,1)S(1)}, bf16[96,896]{1,0:T(8,128)(2,1)S(1)}, u32[]{:S(2)}, u32[]{:S(2)}) collective-permute-start(bf16[96,896]{1,0:T(8,128)(2,1)S(1)} %pad_maximum_fusion.2), channel_id=1, source_target_pairs={{0,8},{8,0},{16,24},{24,16},{32,40},{40,32},{48,56},{56,48},{64,72... | collective-permute-start | bytes 516104 | tf_op jit(solution)/shard_map/ppermute | solution.py:48
  15.7 43.7 %all-to-all-start = ((f32[16,8,128]{2,1,0:T(8,128)}), f32[16,8,128]{2,1,0:T(8,128)S(1)}, u32[]{:S(2)}, u32[]{:S(2)}) async-start(f32[16,8,128]{2,1,0:T(8,128)} %broadcast_in_dim.47), calls=%async_computation | async-start | bytes 131072 | tf_op jit(solution)/shard_map/all_to_all | solution.py:62
  59.4 2.1 collective-permute-start
  61.8 25.3 %all-to-all-done = f32[16,8,128]{2,1,0:T(8,128)S(1)} async-done(((f32[16,8,128]{2,1,0:T(8,128)}), f32[16,8,128]{2,1,0:T(8,128)S(1)}, u32[]{:S(2)}, u32[]{:S(2)}) %all-to-all-start) | async-done | bytes 65568 | tf_op jit(solution)/shard_map/all_to_all | solution.py:62
  87.4 83.9 %all-gather.3.cloned.1.call-done = bf16[2048,896]{1,0:T(8,128)(2,1)} async-done(((bf16[128,896]{1,0:T(8,128)(2,1)}), bf16[2048,896]{1,0:T(8,128)(2,1)}) %all-gather.3.cloned.1.call-update) | async-done | bytes 3670032 | tf_op jit(solution)/shard_map/all_gather | solution.py:55
  171.2 1.9 collective-permute-start.2
  173.2 3.3 convolution_convert_fusion.2
  176.8 2.8 convolution_convert_fusion.3
  179.6 3.6 convolution_convert_fusion
  183.2 1.9 collective-permute-start.1
  185.1 6.2 %collective-permute-done.2 = bf16[896,512]{1,0:T(8,128)(2,1)} collective-permute-done((bf16[896,512]{1,0:T(8,128)(2,1)S(1)}, bf16[896,512]{1,0:T(8,128)(2,1)}, u32[]{:S(2)}, u32[]{:S(2)}) %collective-permute-start.2) | collective-permute-done | bytes 917536 | tf_op jit(solution)/shard_map/ppermute | solution.py:48
  193.1 2.0 collective-permute-start.4
  195.3 2.7 convolution_convert_fusion.4
  200.8 7.0 %all-to-all-start.2 = ((bf16[4,160,512]{2,1,0:T(8,128)(2,1)}), bf16[4,160,512]{2,1,0:T(8,128)(2,1)S(1)}, u32[]{:S(2)}, u32[]{:S(2)}) async-start(bf16[4,160,512]{2,1,0:T(8,128)(2,1)} %add_convert_fusion), calls=%async_computation.2 | async-start | bytes 1310720 | tf_op jit(solution)/shard_map/all_to_all | solution.py:109
  207.8 4.3 %fusion.10 = bf16[4,96,1536]{2,1,0:T(8,128)(2,1)} fusion(bf16[4,96,896]{2,1,0:T(8,128)(2,1)S(1)} %bitcast.65, bf16[4,96,1536]{2,1,0:T(8,128)(2,1)} %collective-permute-done.1, bf16[896,512]{1,0:T(8,128)(2,1)S(1)} %copy-done, bf16[896,512]{1,0:T(8,128)(2,1)} %collective-permute-done, bf16[896,512]{1,0:T(8,128)(2,1)} %param.11), kind=kOutput, calls=%fused_computation.12 | convolution fusion | flops 1068171264 | bytes 5799936 | tf_op jit(solution)/shard_map/jrd,dp->jrp/dot_general | solution.py:15
  212.1 5.8 %all-to-all-done.2 = bf16[4,160,512]{2,1,0:T(8,128)(2,1)S(1)} async-done(((bf16[4,160,512]{2,1,0:T(8,128)(2,1)}), bf16[4,160,512]{2,1,0:T(8,128)(2,1)S(1)}, u32[]{:S(2)}, u32[]{:S(2)}) %all-to-all-start.2) | async-done | bytes 655392 | tf_op jit(solution)/shard_map/all_to_all | solution.py:109
  217.9 5.0 %all-to-all-start.1 = ((bf16[4,96,1536]{2,1,0:T(8,128)(2,1)}), bf16[4,96,1536]{2,1,0:T(8,128)(2,1)S(1)}, u32[]{:S(2)}, u32[]{:S(2)}) async-start(bf16[4,96,1536]{2,1,0:T(8,128)(2,1)} %fusion.10), calls=%async_computation.1 | async-start | bytes 2359296 | tf_op jit(solution)/shard_map/all_to_all | solution.py:109
  222.9 2.2 collective-permute-start.6
  225.3 12.5 %all-to-all-done.1 = bf16[4,96,1536]{2,1,0:T(8,128)(2,1)S(1)} async-done(((bf16[4,96,1536]{2,1,0:T(8,128)(2,1)}), bf16[4,96,1536]{2,1,0:T(8,128)(2,1)S(1)}, u32[]{:S(2)}, u32[]{:S(2)}) %all-to-all-start.1) | async-done | bytes 1179680 | tf_op jit(solution)/shard_map/all_to_all | solution.py:109
  238.1 13.9 %all-gather = bf16[448,1024]{1,0:T(8,128)(2,1)S(1)} all-gather(bf16[112,1024]{1,0:T(8,128)(2,1)S(1)} %pad_maximum_fusion.1), channel_id=2, replica_groups={{0,2,4,6},{1,3,5,7},{8,10,12,14},{9,11,13,15},{16,18,20,22},{17,19,21,2..., dimensions={0}, use_global_device_ids=true | all-gather | bytes 1146880 | tf_op jit(solution)/shard_map/all_gather | solution.py:125
  254.5 3.3 fusion.14
  258.1 2.5 fusion.15
  260.8 2.6 fusion.11
  263.5 112.1 %reduce-scatter.2.cloned.1.call-done = bf16[128,896]{1,0:T(8,128)(2,1)} async-done(((bf16[2048,896]{1,0:T(8,128)(2,1)}), bf16[128,896]{1,0:T(8,128)(2,1)}) %reduce-scatter.2.cloned.1.call-update) | async-done | bytes 229392 | tf_op jit(solution)/shard_map/reduce_scatter | solution.py:143
  (59 shorter events, 13.2 us)
Async XLA Ops:
  6.5 164.7 %copy-start = (bf16[896,512]{1,0:T(8,128)(2,1)S(1)}, bf16[896,512]{1,0:T(8,128)(2,1)}, u32[]{:S(2)}) copy-start(bf16[896,512]{1,0:T(8,128)(2,1)} %param.12) | copy-start | bytes 2752516
  6.5 164.7 %all-gather.3.cloned.1.call-start = ((), (), s32[]{:S(2)}) async-start(), calls=%async_computation.4 | async-start | bytes 3899392 | tf_op jit(solution)/shard_map/all_gather | solution.py:55
  8.3 53.3 %collective-permute-start.3 = (bf16[96,896]{1,0:T(8,128)(2,1)S(1)}, bf16[96,896]{1,0:T(8,128)(2,1)S(1)}, u32[]{:S(2)}, u32[]{:S(2)}) collective-permute-start(bf16[96,896]{1,0:T(8,128)(2,1)S(1)} %pad_maximum_fusion.2), channel_id=1, source_target_pairs={{0,8},{8,0},{16,24},{24,16},{32,40},{40,32},{48,56},{56,48},{64,72... | collective-permute-start | bytes 516104 | tf_op jit(solution)/shard_map/ppermute | solution.py:48
  15.7 71.4 %all-to-all-start = ((f32[16,8,128]{2,1,0:T(8,128)}), f32[16,8,128]{2,1,0:T(8,128)S(1)}, u32[]{:S(2)}, u32[]{:S(2)}) async-start(f32[16,8,128]{2,1,0:T(8,128)} %broadcast_in_dim.47), calls=%async_computation | async-start | bytes 131072 | tf_op jit(solution)/shard_map/all_to_all | solution.py:62
  59.4 120.1 %collective-permute-start = (bf16[896,512]{1,0:T(8,128)(2,1)}, bf16[896,512]{1,0:T(8,128)(2,1)}, u32[]{:S(2)}, u32[]{:S(2)}) collective-permute-start(bf16[896,512]{1,0:T(8,128)(2,1)} %param.11), channel_id=1, source_target_pairs={{0,8},{8,0},{16,24},{24,16},{32,40},{40,32},{48,56},{56,48},{64,72... | collective-permute-start | bytes 2752520 | tf_op jit(solution)/shard_map/ppermute | solution.py:48
  171.2 20.1 %collective-permute-start.2 = (bf16[896,512]{1,0:T(8,128)(2,1)S(1)}, bf16[896,512]{1,0:T(8,128)(2,1)}, u32[]{:S(2)}, u32[]{:S(2)}) collective-permute-start(bf16[896,512]{1,0:T(8,128)(2,1)S(1)} %copy-done), channel_id=1, source_target_pairs={{0,8},{8,0},{16,24},{24,16},{32,40},{40,32},{48,56},{56,48},{64,72... | collective-permute-start | bytes 2752520 | tf_op jit(solution)/shard_map/ppermute | solution.py:48
  176.5 3.0 copy-start.1
  183.2 24.7 %collective-permute-start.1 = (bf16[4,96,1536]{2,1,0:T(8,128)(2,1)}, bf16[4,96,1536]{2,1,0:T(8,128)(2,1)}, u32[]{:S(2)}, u32[]{:S(2)}) collective-permute-start(bf16[4,96,1536]{2,1,0:T(8,128)(2,1)} %convolution_convert_fusion), channel_id=1, source_target_pairs={{0,1},{1,0},{2,3},{3,2},{4,5},{5,4},{6,7},{7,6},{8,9},{9,8},{10,11... | collective-permute-start | bytes 3538952 | tf_op jit(solution)/shard_map/ppermute | solution.py:107
  193.1 6.6 %collective-permute-start.4 = (bf16[4,160,512]{2,1,0:T(8,128)(2,1)S(1)}, bf16[4,160,512]{2,1,0:T(8,128)(2,1)S(1)}, u32[]{:S(2)}, u32[]{:S(2)}) collective-permute-start(bf16[4,160,512]{2,1,0:T(8,128)(2,1)S(1)} %pad_maximum_fusion), channel_id=1, source_target_pairs={{0,1},{1,0},{2,3},{3,2},{4,5},{5,4},{6,7},{7,6},{8,9},{9,8},{10,11... | collective-permute-start | bytes 1966088 | tf_op jit(solution)/shard_map/ppermute | solution.py:107
  200.8 17.1 %all-to-all-start.2 = ((bf16[4,160,512]{2,1,0:T(8,128)(2,1)}), bf16[4,160,512]{2,1,0:T(8,128)(2,1)S(1)}, u32[]{:S(2)}, u32[]{:S(2)}) async-start(bf16[4,160,512]{2,1,0:T(8,128)(2,1)} %add_convert_fusion), calls=%async_computation.2 | async-start | bytes 1310720 | tf_op jit(solution)/shard_map/all_to_all | solution.py:109
  217.9 19.9 %all-to-all-start.1 = ((bf16[4,96,1536]{2,1,0:T(8,128)(2,1)}), bf16[4,96,1536]{2,1,0:T(8,128)(2,1)S(1)}, u32[]{:S(2)}, u32[]{:S(2)}) async-start(bf16[4,96,1536]{2,1,0:T(8,128)(2,1)} %fusion.10), calls=%async_computation.1 | async-start | bytes 2359296 | tf_op jit(solution)/shard_map/all_to_all | solution.py:109
  222.9 152.7 %reduce-scatter.2.cloned.1.call-start = ((), (), s32[]{:S(2)}) async-start(), calls=%async_computation.5 | async-start | bytes 3899392 | tf_op jit(solution)/shard_map/reduce_scatter | solution.py:143
  222.9 31.6 %collective-permute-start.6 = (bf16[512,896]{1,0:T(8,128)(2,1)}, bf16[512,896]{1,0:T(8,128)(2,1)}, u32[]{:S(2)}, u32[]{:S(2)}) collective-permute-start(bf16[512,896]{1,0:T(8,128)(2,1)} %param.13), channel_id=1, source_target_pairs={{0,8},{8,0},{16,24},{24,16},{32,40},{40,32},{48,56},{56,48},{64,72... | collective-permute-start | bytes 2752520 | tf_op jit(solution)/shard_map/ppermute | solution.py:48
  252.0 5.9 %collective-permute-start.5 = (bf16[4,112,1024]{2,1,0:T(8,128)(2,1)S(1)}, bf16[4,112,1024]{2,1,0:T(8,128)(2,1)S(1)}, u32[]{:S(2)}, u32[]{:S(2)}) collective-permute-start(bf16[4,112,1024]{2,1,0:T(8,128)(2,1)S(1)} %bitcast.58), channel_id=1, source_target_pairs={{0,1},{1,0},{2,3},{3,2},{4,5},{5,4},{6,7},{7,6},{8,9},{9,8},{10,11... | collective-permute-start | bytes 2752520 | tf_op jit(solution)/shard_map/ppermute | solution.py:126
  258.1 2.7 copy-start.2
Sparse Core Ops, SparseCore 0:
  9.4 161.7 all-gather.2
  263.6 111.9 reduce-scatter.1

commit v3 on v2

--- a/solution.py
+++ b/solution.py
@@ -84,12 +84,13 @@
     late_up, down, everyone = lax.optimization_barrier((expert_up, expert_down, everyone))
     ups = with_mates(late_up)
     downs = jnp.concatenate(with_mates(down), axis=0)
-    received = [
-        dot("nct,ntd->ncd", picks, everyone.reshape(near, tok, width))
-        .astype(BF)
-        .reshape(chips, rows, width)
-        for picks, _, _ in (mine, other)
-    ]
+    received = dot(
+        "nct,ntd->ncd",
+        jnp.concatenate([other[0], mine[0]], axis=1),
+        everyone.reshape(near, tok, width),
+    ).astype(BF)
+    received = received.reshape(near, CORES, half, width)
+    received = [received[:, 1 - c].reshape(chips, rows, width) for c in range(CORES)]
     wanted = jnp.stack([side_of[2][:2] for side_of in (mine, other)])
     wanted = wanted.reshape(CORES, 2, chips, -1, width).transpose(0, 2, 1, 3, 4)
     shared_sums = dot("hd,td->ht", wanted.reshape(-1, width), everyone).astype(BF)

time: 383 us -> 382 us (level)
  the two profiles are of different devices: /device:TPU:34 before, /device:TPU:36 now
where the time goes in v3:
time: 382 us; the launch traced here: 381 us
  waiting for transfers between devices  247 us (65%)
  starting transfers between devices  72.9 us (19%)
  matrix products  25.3 us (7%)
  blocking collectives  15.3 us (4%)
  between operations  13.9 us (4%)
  other arithmetic  5.15 us (1%)
    reduce_scatter x1, waiting for transfers between devices, local(): lax.psum_scatter(share.astype(BF).reshape(total, width), 'expert', scatte...  111 us
    all_gather x1, waiting for transfers between devices, local(): lax.all_gather(tokens, 'expert', axis=0, tiled=True, axis_index_groups=ri...  84.5 us
    all_to_all x1, starting transfers between devices, local(): lax.all_to_all(jnp.broadcast_to(info[None], (near, *info.shape)), 'expert...  43.7 us
    dot_general x10, matrix products, dot(): return jnp.einsum(spec, a, b, preferred_element_type=F32)  25.3 us
    all_to_all x1, waiting for transfers between devices, local(): lax.all_to_all(jnp.broadcast_to(info[None], (near, *info.shape)), 'expert...  25.2 us
    all_gather x1, blocking collectives, local(): hidden = lax.all_gather(hidden, 'tensor', axis=0, axis_index_groups=crosses)  15.3 us
    all_to_all x2, waiting for transfers between devices, summed(): lax.all_to_all(both, 'tensor', split_axis=0, concat_axis=0, tiled=True, a...  14.7 us
    all_to_all x2, starting transfers between devices, summed(): lax.all_to_all(both, 'tensor', split_axis=0, concat_axis=0, tiled=True, a...  12.4 us
  transfers between devices with their start and end apart: 12, of which 7 were waited for; matrix products, arithmetic and copies ran while one was open for 7% of the time, Pallas kernels for 0%

profile of v3, /device:TPU:36, one launch (start us, length us, event | category | flops | bytes accessed | tf_op | source)
XLA Modules:
  0.0 380.9 jit_solution(8013812378418644535)
XLA Ops:
  8.3 4.7 %collective-permute-start.3 = (bf16[96,896]{1,0:T(8,128)(2,1)S(1)}, bf16[96,896]{1,0:T(8,128)(2,1)S(1)}, u32[]{:S(2)}, u32[]{:S(2)}) collective-permute-start(bf16[96,896]{1,0:T(8,128)(2,1)S(1)} %pad_maximum_fusion.2), channel_id=1, source_target_pairs={{0,8},{8,0},{16,24},{24,16},{32,40},{40,32},{48,56},{56,48},{64,72... | collective-permute-start | bytes 516104 | tf_op jit(solution)/shard_map/ppermute | solution.py:48
  15.7 43.7 %all-to-all-start = ((f32[16,8,128]{2,1,0:T(8,128)}), f32[16,8,128]{2,1,0:T(8,128)S(1)}, u32[]{:S(2)}, u32[]{:S(2)}) async-start(f32[16,8,128]{2,1,0:T(8,128)} %broadcast_in_dim.47), calls=%async_computation | async-start | bytes 131072 | tf_op jit(solution)/shard_map/all_to_all | solution.py:62
  59.4 2.1 collective-permute-start
  61.8 25.2 %all-to-all-done = f32[16,8,128]{2,1,0:T(8,128)S(1)} async-done(((f32[16,8,128]{2,1,0:T(8,128)}), f32[16,8,128]{2,1,0:T(8,128)S(1)}, u32[]{:S(2)}, u32[]{:S(2)}) %all-to-all-start) | async-done | bytes 65568 | tf_op jit(solution)/shard_map/all_to_all | solution.py:62
  87.4 84.5 %all-gather.3.cloned.1.call-done = bf16[2048,896]{1,0:T(8,128)(2,1)} async-done(((bf16[128,896]{1,0:T(8,128)(2,1)}), bf16[2048,896]{1,0:T(8,128)(2,1)}) %all-gather.3.cloned.1.call-update) | async-done | bytes 3670032 | tf_op jit(solution)/shard_map/all_gather | solution.py:55
  171.9 3.4 convolution_convert_fusion.2
  175.5 2.0 collective-permute-start.2
  177.5 2.8 convolution_convert_fusion.3
  180.4 3.6 convolution_convert_fusion
  184.0 1.9 collective-permute-start.1
  186.0 9.8 %collective-permute-done.2 = bf16[896,512]{1,0:T(8,128)(2,1)S(1)} collective-permute-done((bf16[896,512]{1,0:T(8,128)(2,1)S(1)}, bf16[896,512]{1,0:T(8,128)(2,1)S(1)}, u32[]{:S(2)}, u32[]{:S(2)}) %collective-permute-start.2) | collective-permute-done | bytes 917536 | tf_op jit(solution)/shard_map/ppermute | solution.py:48
  196.4 2.0 collective-permute-start.4
  201.5 5.9 %all-to-all-start.2 = ((bf16[4,160,512]{2,1,0:T(8,128)(2,1)}), bf16[4,160,512]{2,1,0:T(8,128)(2,1)S(1)}, u32[]{:S(2)}, u32[]{:S(2)}) async-start(bf16[4,160,512]{2,1,0:T(8,128)(2,1)} %add_convert_fusion), calls=%async_computation.2 | async-start | bytes 1310720 | tf_op jit(solution)/shard_map/all_to_all | solution.py:110
  207.4 4.5 %fusion.10 = bf16[4,96,1536]{2,1,0:T(8,128)(2,1)} fusion(bf16[4,96,896]{2,1,0:T(8,128)(2,1)S(1)} %bitcast.65, bf16[4,96,1536]{2,1,0:T(8,128)(2,1)} %collective-permute-done.1, bf16[896,512]{1,0:T(8,128)(2,1)} %param.12, bf16[896,512]{1,0:T(8,128)(2,1)} %collective-permute-done, bf16[896,512]{1,0:T(8,128)(2,1)} %param.11), kind=kOutput, calls=%fused_computation.12 | convolution fusion | flops 1068171264 | bytes 5799936 | tf_op jit(solution)/shard_map/jrd,dp->jrp/dot_general | solution.py:15
  211.9 3.9 %all-to-all-done.2 = bf16[4,160,512]{2,1,0:T(8,128)(2,1)S(1)} async-done(((bf16[4,160,512]{2,1,0:T(8,128)(2,1)}), bf16[4,160,512]{2,1,0:T(8,128)(2,1)S(1)}, u32[]{:S(2)}, u32[]{:S(2)}) %all-to-all-start.2) | async-done | bytes 655392 | tf_op jit(solution)/shard_map/all_to_all | solution.py:110
  215.9 6.5 %all-to-all-start.1 = ((bf16[4,96,1536]{2,1,0:T(8,128)(2,1)}), bf16[4,96,1536]{2,1,0:T(8,128)(2,1)S(1)}, u32[]{:S(2)}, u32[]{:S(2)}) async-start(bf16[4,96,1536]{2,1,0:T(8,128)(2,1)} %fusion.10), calls=%async_computation.1 | async-start | bytes 2359296 | tf_op jit(solution)/shard_map/all_to_all | solution.py:110
  222.4 2.2 collective-permute-start.6
  224.8 10.8 %all-to-all-done.1 = bf16[4,96,1536]{2,1,0:T(8,128)(2,1)S(1)} async-done(((bf16[4,96,1536]{2,1,0:T(8,128)(2,1)}), bf16[4,96,1536]{2,1,0:T(8,128)(2,1)S(1)}, u32[]{:S(2)}, u32[]{:S(2)}) %all-to-all-start.1) | async-done | bytes 1179680 | tf_op jit(solution)/shard_map/all_to_all | solution.py:110
  235.9 15.3 %all-gather = bf16[448,1024]{1,0:T(8,128)(2,1)S(1)} all-gather(bf16[112,1024]{1,0:T(8,128)(2,1)S(1)} %pad_maximum_fusion.1), channel_id=2, replica_groups={{0,2,4,6},{1,3,5,7},{8,10,12,14},{9,11,13,15},{16,18,20,22},{17,19,21,2..., dimensions={0}, use_global_device_ids=true | all-gather | bytes 1146880 | tf_op jit(solution)/shard_map/all_gather | solution.py:126
  251.2 1.9 collective-permute-start.5
  253.6 3.3 fusion.14
  257.2 2.5 fusion.15
  259.9 2.7 fusion.11
  262.6 111.4 %reduce-scatter.2.cloned.1.call-done = bf16[128,896]{1,0:T(8,128)(2,1)} async-done(((bf16[2048,896]{1,0:T(8,128)(2,1)}), bf16[128,896]{1,0:T(8,128)(2,1)}) %reduce-scatter.2.cloned.1.call-update) | async-done | bytes 229392 | tf_op jit(solution)/shard_map/reduce_scatter | solution.py:144
  (61 shorter events, 10.3 us)
Async XLA Ops:
  6.5 165.3 %all-gather.3.cloned.1.call-start = ((), (), s32[]{:S(2)}) async-start(), calls=%async_computation.4 | async-start | bytes 3899392 | tf_op jit(solution)/shard_map/all_gather | solution.py:55
  8.3 53.3 %collective-permute-start.3 = (bf16[96,896]{1,0:T(8,128)(2,1)S(1)}, bf16[96,896]{1,0:T(8,128)(2,1)S(1)}, u32[]{:S(2)}, u32[]{:S(2)}) collective-permute-start(bf16[96,896]{1,0:T(8,128)(2,1)S(1)} %pad_maximum_fusion.2), channel_id=1, source_target_pairs={{0,8},{8,0},{16,24},{24,16},{32,40},{40,32},{48,56},{56,48},{64,72... | collective-permute-start | bytes 516104 | tf_op jit(solution)/shard_map/ppermute | solution.py:48
  15.7 71.4 %all-to-all-start = ((f32[16,8,128]{2,1,0:T(8,128)}), f32[16,8,128]{2,1,0:T(8,128)S(1)}, u32[]{:S(2)}, u32[]{:S(2)}) async-start(f32[16,8,128]{2,1,0:T(8,128)} %broadcast_in_dim.47), calls=%async_computation | async-start | bytes 131072 | tf_op jit(solution)/shard_map/all_to_all | solution.py:62
  59.4 121.0 %collective-permute-start = (bf16[896,512]{1,0:T(8,128)(2,1)}, bf16[896,512]{1,0:T(8,128)(2,1)}, u32[]{:S(2)}, u32[]{:S(2)}) collective-permute-start(bf16[896,512]{1,0:T(8,128)(2,1)} %param.11), channel_id=1, source_target_pairs={{0,8},{8,0},{16,24},{24,16},{32,40},{40,32},{48,56},{56,48},{64,72... | collective-permute-start | bytes 2752520 | tf_op jit(solution)/shard_map/ppermute | solution.py:48
  171.9 3.6 copy-start
  175.5 20.3 %collective-permute-start.2 = (bf16[896,512]{1,0:T(8,128)(2,1)S(1)}, bf16[896,512]{1,0:T(8,128)(2,1)S(1)}, u32[]{:S(2)}, u32[]{:S(2)}) collective-permute-start(bf16[896,512]{1,0:T(8,128)(2,1)S(1)} %copy-done), channel_id=1, source_target_pairs={{0,8},{8,0},{16,24},{24,16},{32,40},{40,32},{48,56},{56,48},{64,72... | collective-permute-start | bytes 2752520 | tf_op jit(solution)/shard_map/ppermute | solution.py:48
  177.5 3.0 copy-start.1
  184.0 23.4 %collective-permute-start.1 = (bf16[4,96,1536]{2,1,0:T(8,128)(2,1)}, bf16[4,96,1536]{2,1,0:T(8,128)(2,1)}, u32[]{:S(2)}, u32[]{:S(2)}) collective-permute-start(bf16[4,96,1536]{2,1,0:T(8,128)(2,1)} %convolution_convert_fusion), channel_id=1, source_target_pairs={{0,1},{1,0},{2,3},{3,2},{4,5},{5,4},{6,7},{7,6},{8,9},{9,8},{10,11... | collective-permute-start | bytes 3538952 | tf_op jit(solution)/shard_map/ppermute | solution.py:108
  195.8 2.6 copy-start.2
  196.4 4.0 %collective-permute-start.4 = (bf16[4,160,512]{2,1,0:T(8,128)(2,1)S(1)}, bf16[4,160,512]{2,1,0:T(8,128)(2,1)S(1)}, u32[]{:S(2)}, u32[]{:S(2)}) collective-permute-start(bf16[4,160,512]{2,1,0:T(8,128)(2,1)S(1)} %pad_maximum_fusion), channel_id=1, source_target_pairs={{0,1},{1,0},{2,3},{3,2},{4,5},{5,4},{6,7},{7,6},{8,9},{9,8},{10,11... | collective-permute-start | bytes 1966088 | tf_op jit(solution)/shard_map/ppermute | solution.py:108
  201.5 14.4 %all-to-all-start.2 = ((bf16[4,160,512]{2,1,0:T(8,128)(2,1)}), bf16[4,160,512]{2,1,0:T(8,128)(2,1)S(1)}, u32[]{:S(2)}, u32[]{:S(2)}) async-start(bf16[4,160,512]{2,1,0:T(8,128)(2,1)} %add_convert_fusion), calls=%async_computation.2 | async-start | bytes 1310720 | tf_op jit(solution)/shard_map/all_to_all | solution.py:110
  215.9 19.7 %all-to-all-start.1 = ((bf16[4,96,1536]{2,1,0:T(8,128)(2,1)}), bf16[4,96,1536]{2,1,0:T(8,128)(2,1)S(1)}, u32[]{:S(2)}, u32[]{:S(2)}) async-start(bf16[4,96,1536]{2,1,0:T(8,128)(2,1)} %fusion.10), calls=%async_computation.1 | async-start | bytes 2359296 | tf_op jit(solution)/shard_map/all_to_all | solution.py:110
  222.4 151.7 %reduce-scatter.2.cloned.1.call-start = ((), (), s32[]{:S(2)}) async-start(), calls=%async_computation.5 | async-start | bytes 3899392 | tf_op jit(solution)/shard_map/reduce_scatter | solution.py:144
  222.4 31.3 %collective-permute-start.6 = (bf16[512,896]{1,0:T(8,128)(2,1)}, bf16[512,896]{1,0:T(8,128)(2,1)}, u32[]{:S(2)}, u32[]{:S(2)}) collective-permute-start(bf16[512,896]{1,0:T(8,128)(2,1)} %param.13), channel_id=1, source_target_pairs={{0,8},{8,0},{16,24},{24,16},{32,40},{40,32},{48,56},{56,48},{64,72... | collective-permute-start | bytes 2752520 | tf_op jit(solution)/shard_map/ppermute | solution.py:48
  251.2 5.8 %collective-permute-start.5 = (bf16[4,112,1024]{2,1,0:T(8,128)(2,1)S(1)}, bf16[4,112,1024]{2,1,0:T(8,128)(2,1)S(1)}, u32[]{:S(2)}, u32[]{:S(2)}) collective-permute-start(bf16[4,112,1024]{2,1,0:T(8,128)(2,1)S(1)} %bitcast.58), channel_id=1, source_target_pairs={{0,1},{1,0},{2,3},{3,2},{4,5},{5,4},{6,7},{7,6},{8,9},{9,8},{10,11... | collective-permute-start | bytes 2752520 | tf_op jit(solution)/shard_map/ppermute | solution.py:127
  257.2 2.7 copy-start.3
Sparse Core Ops, SparseCore 0:
  9.4 162.3 all-gather.2
  262.7 111.2 reduce-scatter.1

commit v4 on v3

--- a/solution.py
+++ b/solution.py
@@ -94,15 +94,14 @@
     wanted = jnp.stack([side_of[2][:2] for side_of in (mine, other)])
     wanted = wanted.reshape(CORES, 2, chips, -1, width).transpose(0, 2, 1, 3, 4)
     shared_sums = dot("hd,td->ht", wanted.reshape(-1, width), everyone).astype(BF)
-    shared_sums = shared_sums.reshape(CORES, chips, -1, columns)
+    shared_sums = shared_sums.reshape(CORES, chips, -1, FFE)
 
     def first(which):
-        weights = jnp.concatenate([*gates, expert_up], axis=1)
-        return dot("jrd,dp->jrp", received[which], weights).astype(BF)
+        return dot("jrd,dp->jrp", received[which], jnp.concatenate(gates, axis=1)).astype(BF)
 
     def second(which):
-        late = [dot("jrd,dp->jrp", received[which], up).astype(BF) for up in ups[1:]]
-        return jnp.concatenate([*late, shared_sums[which]], axis=1)
+        late = dot("jrd,dp->jrp", received[which], jnp.concatenate(ups, axis=1)).astype(BF)
+        return jnp.concatenate([late, shared_sums[which]], axis=1)
 
     def summed(partials):
         theirs = lax.ppermute(partials(1), "tensor", partner)
@@ -113,14 +112,8 @@
         return jnp.sum(crossed.astype(F32), axis=0)
 
     early, late = summed(first), summed(second)
-    gate_of, up_of = early[:, :FFE], [early[:, FFE:]]
-    up_of += [late[rows * p : rows * (p + 1)] for p in range(pieces - 1)]
-    pair = late[rows * (pieces - 1) :].reshape(2, -1, total)
-    routed = [
-        (jax.nn.silu(gate_of[:, columns * p : columns * (p + 1)]) * up_of[p]).astype(BF)
-        for p in range(pieces)
-    ]
-    routed = jnp.concatenate(routed, axis=1)
+    routed = (jax.nn.silu(early) * late[:rows]).astype(BF)
+    pair = late[rows:].reshape(2, -1, total)
     shared_hidden = (jax.nn.silu(pair[0]) * pair[1]).astype(BF).reshape(-1, FFE)
     hidden = jnp.concatenate([routed, shared_hidden], axis=0)
     hidden = lax.all_gather(hidden, "tensor", axis=0, axis_index_groups=crosses)

time: 382 us -> 379 us (level)
  the two profiles are of different devices: /device:TPU:36 before, /device:TPU:44 now
where the time goes in v4:
time: 379 us; the launch traced here: 378 us
  waiting for transfers between devices  244 us (64%)
  starting transfers between devices  71.8 us (19%)
  matrix products  21.5 us (6%)
  blocking collectives  15.4 us (4%)
  between operations  13.9 us (4%)
  other arithmetic  6.85 us (2%)
  local copies, waits for them, and re-layouts  4.28 us (1%)
    reduce_scatter x1, waiting for transfers between devices, local(): lax.psum_scatter(share.astype(BF).reshape(total, width), 'expert', scatte...  113 us
    all_gather x1, waiting for transfers between devices, local(): lax.all_gather(tokens, 'expert', axis=0, tiled=True, axis_index_groups=ri...  81.7 us
    all_to_all x1, starting transfers between devices, local(): lax.all_to_all(jnp.broadcast_to(info[None], (near, *info.shape)), 'expert...  43.7 us
    all_to_all x1, waiting for transfers between devices, local(): lax.all_to_all(jnp.broadcast_to(info[None], (near, *info.shape)), 'expert...  24.8 us
    dot_general x10, matrix products, dot(): return jnp.einsum(spec, a, b, preferred_element_type=F32)  21.5 us
    all_gather x1, blocking collectives, local(): hidden = lax.all_gather(hidden, 'tensor', axis=0, axis_index_groups=crosses)  15.4 us
    all_to_all x2, waiting for transfers between devices, summed(): lax.all_to_all(both, 'tensor', split_axis=0, concat_axis=0, tiled=True, a...  15.4 us
    all_to_all x2, starting transfers between devices, summed(): lax.all_to_all(both, 'tensor', split_axis=0, concat_axis=0, tiled=True, a...  11.3 us
  transfers between devices with their start and end apart: 12, of which 6 were waited for; matrix products, arithmetic and copies ran while one was open for 7% of the time, Pallas kernels for 0%

profile of v4, /device:TPU:44, one launch (start us, length us, event | category | flops | bytes accessed | tf_op | source)
XLA Modules:
  0.0 378.1 jit_solution(11741616221922696135)
XLA Ops:
  8.3 4.7 %collective-permute-start.3 = (bf16[96,896]{1,0:T(8,128)(2,1)S(1)}, bf16[96,896]{1,0:T(8,128)(2,1)S(1)}, u32[]{:S(2)}, u32[]{:S(2)}) collective-permute-start(bf16[96,896]{1,0:T(8,128)(2,1)S(1)} %pad_maximum_fusion.2), channel_id=1, source_target_pairs={{0,8},{8,0},{16,24},{24,16},{32,40},{40,32},{48,56},{56,48},{64,72... | collective-permute-start | bytes 516104 | tf_op jit(solution)/shard_map/ppermute | solution.py:48
  15.7 43.7 %all-to-all-start = ((f32[16,8,128]{2,1,0:T(8,128)}), f32[16,8,128]{2,1,0:T(8,128)S(1)}, u32[]{:S(2)}, u32[]{:S(2)}) async-start(f32[16,8,128]{2,1,0:T(8,128)} %broadcast_in_dim.47), calls=%async_computation | async-start | bytes 131072 | tf_op jit(solution)/shard_map/all_to_all | solution.py:62
  59.4 2.1 collective-permute-start
  62.5 24.8 %all-to-all-done = f32[16,8,128]{2,1,0:T(8,128)S(1)} async-done(((f32[16,8,128]{2,1,0:T(8,128)}), f32[16,8,128]{2,1,0:T(8,128)S(1)}, u32[]{:S(2)}, u32[]{:S(2)}) %all-to-all-start) | async-done | bytes 65568 | tf_op jit(solution)/shard_map/all_to_all | solution.py:62
  87.6 81.7 %all-gather.3.cloned.1.call-done = bf16[2048,896]{1,0:T(8,128)(2,1)} async-done(((bf16[128,896]{1,0:T(8,128)(2,1)}), bf16[2048,896]{1,0:T(8,128)(2,1)}) %all-gather.3.cloned.1.call-update) | async-done | bytes 3670032 | tf_op jit(solution)/shard_map/all_gather | solution.py:55
  169.3 1.9 collective-permute-start.2
  171.2 3.3 convolution_convert_fusion
  174.7 2.7 convolution_convert_fusion.1
  179.9 2.0 collective-permute-start.1
  181.8 9.2 %collective-permute-done.2 = bf16[896,512]{1,0:T(8,128)(2,1)} collective-permute-done((bf16[896,512]{1,0:T(8,128)(2,1)S(1)}, bf16[896,512]{1,0:T(8,128)(2,1)}, u32[]{:S(2)}, u32[]{:S(2)}) %collective-permute-start.2) | collective-permute-done | bytes 917536 | tf_op jit(solution)/shard_map/ppermute | solution.py:48
  191.0 2.2 convolution_convert_fusion.2
  193.3 2.0 collective-permute-start.4
  197.5 4.8 %all-to-all-start.1 = ((bf16[4,96,1024]{2,1,0:T(8,128)(2,1)}), bf16[4,96,1024]{2,1,0:T(8,128)(2,1)S(1)}, u32[]{:S(2)}, u32[]{:S(2)}) async-start(bf16[4,96,1024]{2,1,0:T(8,128)(2,1)} %add_convert_fusion.1), calls=%async_computation.1 | async-start | bytes 1572864 | tf_op jit(solution)/shard_map/all_to_all | solution.py:109
  202.4 2.6 convolution_convert_fusion.3
  206.5 5.8 %all-to-all-done.1 = bf16[4,96,1024]{2,1,0:T(8,128)(2,1)S(1)} async-done(((bf16[4,96,1024]{2,1,0:T(8,128)(2,1)}), bf16[4,96,1024]{2,1,0:T(8,128)(2,1)S(1)}, u32[]{:S(2)}, u32[]{:S(2)}) %all-to-all-start.1) | async-done | bytes 786464 | tf_op jit(solution)/shard_map/all_to_all | solution.py:109
  212.3 6.5 %all-to-all-start.2 = ((bf16[4,128,1024]{2,1,0:T(8,128)(2,1)}), bf16[4,128,1024]{2,1,0:T(8,128)(2,1)S(1)}, u32[]{:S(2)}, u32[]{:S(2)}) async-start(bf16[4,128,1024]{2,1,0:T(8,128)(2,1)} %add_convert_fusion), calls=%async_computation.2 | async-start | bytes 2097152 | tf_op jit(solution)/shard_map/all_to_all | solution.py:109
  218.8 2.2 collective-permute-start.6
  221.2 9.5 %all-to-all-done.2 = bf16[4,128,1024]{2,1,0:T(8,128)(2,1)S(1)} async-done(((bf16[4,128,1024]{2,1,0:T(8,128)(2,1)}), bf16[4,128,1024]{2,1,0:T(8,128)(2,1)S(1)}, u32[]{:S(2)}, u32[]{:S(2)}) %all-to-all-start.2) | async-done | bytes 1048608 | tf_op jit(solution)/shard_map/all_to_all | solution.py:109
  231.1 15.4 %all-gather = bf16[448,1024]{1,0:T(8,128)(2,1)S(1)} all-gather(bf16[112,1024]{1,0:T(8,128)(2,1)S(1)} %pad_maximum_fusion.1), channel_id=2, replica_groups={{0,2,4,6},{1,3,5,7},{8,10,12,14},{9,11,13,15},{16,18,20,22},{17,19,21,2..., dimensions={0}, use_global_device_ids=true | all-gather | bytes 1146880 | tf_op jit(solution)/shard_map/all_gather | solution.py:119
  246.5 1.9 collective-permute-start.5
  249.7 3.3 fusion.11
  253.3 2.5 fusion.12
  256.0 2.7 fusion.8
  258.7 112.5 %reduce-scatter.2.cloned.1.call-done = bf16[128,896]{1,0:T(8,128)(2,1)} async-done(((bf16[2048,896]{1,0:T(8,128)(2,1)}), bf16[128,896]{1,0:T(8,128)(2,1)}) %reduce-scatter.2.cloned.1.call-update) | async-done | bytes 229392 | tf_op jit(solution)/shard_map/reduce_scatter | solution.py:137
  (67 shorter events, 14.0 us)
Async XLA Ops:
  6.5 162.7 %copy-start.6 = (bf16[896,512]{1,0:T(8,128)(2,1)S(1)}, bf16[896,512]{1,0:T(8,128)(2,1)}, u32[]{:S(2)}) copy-start(bf16[896,512]{1,0:T(8,128)(2,1)} %param.12) | copy-start | bytes 2752516
  6.5 162.7 %all-gather.3.cloned.1.call-start = ((), (), s32[]{:S(2)}) async-start(), calls=%async_computation.4 | async-start | bytes 3899392 | tf_op jit(solution)/shard_map/all_gather | solution.py:55
  8.3 53.3 %collective-permute-start.3 = (bf16[96,896]{1,0:T(8,128)(2,1)S(1)}, bf16[96,896]{1,0:T(8,128)(2,1)S(1)}, u32[]{:S(2)}, u32[]{:S(2)}) collective-permute-start(bf16[96,896]{1,0:T(8,128)(2,1)S(1)} %pad_maximum_fusion.2), channel_id=1, source_target_pairs={{0,8},{8,0},{16,24},{24,16},{32,40},{40,32},{48,56},{56,48},{64,72... | collective-permute-start | bytes 516104 | tf_op jit(solution)/shard_map/ppermute | solution.py:48
  15.7 71.5 %all-to-all-start = ((f32[16,8,128]{2,1,0:T(8,128)}), f32[16,8,128]{2,1,0:T(8,128)S(1)}, u32[]{:S(2)}, u32[]{:S(2)}) async-start(f32[16,8,128]{2,1,0:T(8,128)} %broadcast_in_dim.47), calls=%async_computation | async-start | bytes 131072 | tf_op jit(solution)/shard_map/all_to_all | solution.py:62
  59.4 118.2 %collective-permute-start = (bf16[896,512]{1,0:T(8,128)(2,1)}, bf16[896,512]{1,0:T(8,128)(2,1)S(1)}, u32[]{:S(2)}, u32[]{:S(2)}) collective-permute-start(bf16[896,512]{1,0:T(8,128)(2,1)} %param.11), channel_id=1, source_target_pairs={{0,8},{8,0},{16,24},{24,16},{32,40},{40,32},{48,56},{56,48},{64,72... | collective-permute-start | bytes 2752520 | tf_op jit(solution)/shard_map/ppermute | solution.py:48
  61.7 0.7 copy-start
  61.7 0.7 copy-start.1
  87.6 87.1 %copy-start.3 = (bf16[16,24,128]{2,1,0:T(8,128)(2,1)}, bf16[16,24,128]{2,1,0:T(8,128)(2,1)S(1)}, u32[]{:S(2)}) copy-start(bf16[16,24,128]{2,1,0:T(8,128)(2,1)S(1)} %get-tuple-element.22) | copy-start | bytes 294916
  169.3 21.8 %collective-permute-start.2 = (bf16[896,512]{1,0:T(8,128)(2,1)S(1)}, bf16[896,512]{1,0:T(8,128)(2,1)}, u32[]{:S(2)}, u32[]{:S(2)}) collective-permute-start(bf16[896,512]{1,0:T(8,128)(2,1)S(1)} %copy-done.6), channel_id=1, source_target_pairs={{0,8},{8,0},{16,24},{24,16},{32,40},{40,32},{48,56},{56,48},{64,72... | collective-permute-start | bytes 2752520 | tf_op jit(solution)/shard_map/ppermute | solution.py:48
  177.5 1.4 copy-start.5
  177.6 17.7 %copy-start.2 = (bf16[16,1,24,896]{3,2,1,0:T(8,128)(2,1)}, bf16[16,1,24,896]{3,2,1,0:T(8,128)(2,1)S(1)}, u32[]{:S(2)}) copy-start(bf16[16,1,24,896]{3,2,1,0:T(8,128)(2,1)S(1)} %get-tuple-element.15) | copy-start | bytes 2064388
  179.9 16.4 %collective-permute-start.1 = (bf16[4,96,1024]{2,1,0:T(8,128)(2,1)S(1)}, bf16[4,96,1024]{2,1,0:T(8,128)(2,1)S(1)}, u32[]{:S(2)}, u32[]{:S(2)}) collective-permute-start(bf16[4,96,1024]{2,1,0:T(8,128)(2,1)S(1)} %convolution_convert_fusion.4), channel_id=1, source_target_pairs={{0,1},{1,0},{2,3},{3,2},{4,5},{5,4},{6,7},{7,6},{8,9},{9,8},{10,11... | collective-permute-start | bytes 2359304 | tf_op jit(solution)/shard_map/ppermute | solution.py:107
  193.3 11.8 %collective-permute-start.4 = (bf16[4,128,1024]{2,1,0:T(8,128)(2,1)S(1)}, bf16[4,128,1024]{2,1,0:T(8,128)(2,1)S(1)}, u32[]{:S(2)}, u32[]{:S(2)}) collective-permute-start(bf16[4,128,1024]{2,1,0:T(8,128)(2,1)S(1)} %pad_maximum_fusion), channel_id=1, source_target_pairs={{0,1},{1,0},{2,3},{3,2},{4,5},{5,4},{6,7},{7,6},{8,9},{9,8},{10,11... | collective-permute-start | bytes 3145736 | tf_op jit(solution)/shard_map/ppermute | solution.py:107
  197.5 14.8 %all-to-all-start.1 = ((bf16[4,96,1024]{2,1,0:T(8,128)(2,1)}), bf16[4,96,1024]{2,1,0:T(8,128)(2,1)S(1)}, u32[]{:S(2)}, u32[]{:S(2)}) async-start(bf16[4,96,1024]{2,1,0:T(8,128)(2,1)} %add_convert_fusion.1), calls=%async_computation.1 | async-start | bytes 1572864 | tf_op jit(solution)/shard_map/all_to_all | solution.py:109
  212.3 18.4 %all-to-all-start.2 = ((bf16[4,128,1024]{2,1,0:T(8,128)(2,1)}), bf16[4,128,1024]{2,1,0:T(8,128)(2,1)S(1)}, u32[]{:S(2)}, u32[]{:S(2)}) async-start(bf16[4,128,1024]{2,1,0:T(8,128)(2,1)} %add_convert_fusion), calls=%async_computation.2 | async-start | bytes 2097152 | tf_op jit(solution)/shard_map/all_to_all | solution.py:109
  218.8 152.5 %reduce-scatter.2.cloned.1.call-start = ((), (), s32[]{:S(2)}) async-start(), calls=%async_computation.5 | async-start | bytes 3899392 | tf_op jit(solution)/shard_map/reduce_scatter | solution.py:137
  218.8 31.0 %collective-permute-start.6 = (bf16[512,896]{1,0:T(8,128)(2,1)}, bf16[512,896]{1,0:T(8,128)(2,1)}, u32[]{:S(2)}, u32[]{:S(2)}) collective-permute-start(bf16[512,896]{1,0:T(8,128)(2,1)} %param.13), channel_id=1, source_target_pairs={{0,8},{8,0},{16,24},{24,16},{32,40},{40,32},{48,56},{56,48},{64,72... | collective-permute-start | bytes 2752520 | tf_op jit(solution)/shard_map/ppermute | solution.py:48
  246.5 6.6 %collective-permute-start.5 = (bf16[4,112,1024]{2,1,0:T(8,128)(2,1)S(1)}, bf16[4,112,1024]{2,1,0:T(8,128)(2,1)S(1)}, u32[]{:S(2)}, u32[]{:S(2)}) collective-permute-start(bf16[4,112,1024]{2,1,0:T(8,128)(2,1)S(1)} %bitcast.57), channel_id=1, source_target_pairs={{0,1},{1,0},{2,3},{3,2},{4,5},{5,4},{6,7},{7,6},{8,9},{9,8},{10,11... | collective-permute-start | bytes 2752520 | tf_op jit(solution)/shard_map/ppermute | solution.py:120
  253.3 2.7 copy-start.4
  253.3 2.7 copy-start.7
Sparse Core Ops, SparseCore 0:
  9.4 159.7 all-gather.2
  258.8 112.3 reduce-scatter.1
